TPU v7x, 128 devices: a whole 4x4x4 slice. The times are simulated.
128 devices in a mesh: data: 128 (over z, y, x, core).
Axes of the slice: x: 4, y: 4, z: 4, core: 2. Of those that a mesh axis runs over, the one named last changes fastest.
Arguments:
- x_tokens: bfloat16 [131072, 384], P('data')
- labels: int32 [3, 131072], P(None, 'data')
- w_up: bfloat16 [4, 384, 1536], replicated
- w_down: bfloat16 [4, 1536, 384], replicated
- task_heads: bfloat16 [3, 384, 13], replicated
Outputs:
- output 1: float32 [3], replicated
- output 2: float32 [3, 3], replicated
- output 3: float32 [4, 589824], P(None, 'data')
- output 4: float32 [4, 589824], P(None, 'data')
All inputs are finite; a program needn't handle non-finite values.
Results may differ from a plain program's by a relative error of at most 0.001.
Values are sent between devices in bfloat16 or wider.
A program may use at most 1 GiB of HBM per device.

v0:
```python
import jax
import jax.numpy as jnp
from jax import lax
from jax.sharding import PartitionSpec as P

EG_STEPS = 20


def simplex_weights(gram_mat):
    num_tasks = gram_mat.shape[0]
    value_a11 = jnp.trace(gram_mat) / num_tasks
    alpha_vec = jnp.full((num_tasks,), 1.0 / num_tasks, jnp.float32)
    for step_idx in range(EG_STEPS):
        grad_pull = jnp.sum(gram_mat * alpha_vec[None, :], axis=1)
        alpha_vec = alpha_vec * jnp.exp(-grad_pull / value_a11)
        alpha_vec = alpha_vec / jnp.sum(alpha_vec)
    return alpha_vec


def solution(mesh):
    num_dev = mesh.shape['data']

    def scatter_sum(part_grad, inv_tokens):
        num_tasks = part_grad.shape[0]
        flat_part = (part_grad.reshape(num_tasks, -1) * inv_tokens).astype(jnp.bfloat16)
        received = lax.all_to_all(flat_part, 'data', 1, 0, tiled=True)
        received = received.reshape(num_dev, num_tasks, -1)
        return jnp.sum(received, axis=0, dtype=jnp.float32)

    def local_step(x_local, lab_local, w_up, w_down, task_heads):
        num_layers = w_up.shape[0]
        num_classes = task_heads.shape[2]
        inv_tokens = 1.0 / (x_local.shape[0] * num_dev)
        hidden = x_local
        saved_acts = []
        for layer_idx in range(num_layers):
            pre_act = jnp.dot(hidden, w_up[layer_idx], preferred_element_type=jnp.float32)
            act_val, gelu_slope = jax.jvp(jax.nn.gelu, (pre_act,), (jnp.ones_like(pre_act),))
            act_bf = act_val.astype(jnp.bfloat16)
            mlp_out = jnp.dot(act_bf, w_down[layer_idx], preferred_element_type=jnp.float32)
            saved_acts.append((hidden, act_bf, gelu_slope))
            hidden = (hidden.astype(jnp.float32) + mlp_out).astype(jnp.bfloat16)
        logits = jnp.einsum('bd,tdc->tbc', hidden, task_heads, preferred_element_type=jnp.float32)
        soft_probs = jax.nn.softmax(logits, axis=-1)
        onehot = (lab_local[:, :, None] == jnp.arange(num_classes)[None, None, :]).astype(jnp.float32)
        head_err = (soft_probs - onehot).astype(jnp.bfloat16)
        d_hidden = jnp.einsum('tbc,tdc->tbd', head_err, task_heads, preferred_element_type=jnp.float32).astype(jnp.bfloat16)
        up_shards = [None] * num_layers
        down_shards = [None] * num_layers
        for layer_idx in range(num_layers - 1, -1, -1):
            hidden_in, act_bf, gelu_slope = saved_acts[layer_idx]
            down_grad = jnp.einsum('bf,tbd->tfd', act_bf, d_hidden, preferred_element_type=jnp.float32)
            down_shards[layer_idx] = scatter_sum(down_grad, inv_tokens)
            d_act = jnp.einsum('tbd,fd->tbf', d_hidden, w_down[layer_idx], preferred_element_type=jnp.float32)
            d_pre = (d_act * gelu_slope[None]).astype(jnp.bfloat16)
            up_grad = jnp.einsum('bd,tbf->tdf', hidden_in, d_pre, preferred_element_type=jnp.float32)
            up_shards[layer_idx] = scatter_sum(up_grad, inv_tokens)
            if layer_idx > 0:
                d_hidden = (d_hidden.astype(jnp.float32) + jnp.einsum('tbf,df->tbd', d_pre, w_up[layer_idx], preferred_element_type=jnp.float32)).astype(jnp.bfloat16)
        gram_part = sum(jnp.einsum('ts,us->tu', grad_shard, grad_shard, precision=lax.Precision.HIGHEST, preferred_element_type=jnp.float32) for grad_shard in up_shards + down_shards)
        gram_mat = lax.psum(gram_part, 'data')
        task_weights = simplex_weights(gram_mat)
        grad_up = jnp.stack([jnp.sum(task_weights[:, None] * grad_shard, axis=0) for grad_shard in up_shards])
        grad_down = jnp.stack([jnp.sum(task_weights[:, None] * grad_shard, axis=0) for grad_shard in down_shards])
        return task_weights, gram_mat, grad_up, grad_down

    return jax.shard_map(local_step, mesh=mesh, in_specs=(P('data', None), P(None, 'data'), P(), P(), P()), out_specs=(P(), P(), P(None, 'data'), P(None, 'data')), check_vma=False)
```

profile of v0, /device:TPU:1, one launch (start us, length us, event | category | flops | bytes accessed | tf_op | source)
XLA Modules:
  0.0 792.9 jit_solution(206972697252434001)
XLA Ops:
  0.7 8.5 %fusion.12 = (f32[1024,1536]{1,0:T(8,128)}, f32[1024,1536]{1,0:T(8,128)S(1)}) fusion(bf16[1024,384]{1,0:T(8,128)(2,1)} %param.5, bf16[4,384,1536]{2,1,0:T(8,128)(2,1)} %param.7), kind=kOutput, calls=%fused_computation.40 | convolution fusion | flops 1233125376 | bytes 14548992 | tf_op jit(solution)/shard_map/dot_general | solution.py:37
  28.8 6.7 fusion.42
  41.9 7.6 multiply_convert_fusion.3
  53.2 6.6 fusion.48
  65.8 6.2 convert_element_type.226
  72.0 7.1 copy.68
  79.1 12.2 %all-to-all-start.3 = ((bf16[3,128,4608]{2,0,1:T(4,128)(2,1)}), bf16[3,128,4608]{2,0,1:T(4,128)(2,1)}, u32[]{:S(2)}, u32[]{:S(2)}) async-start(bf16[3,128,4608]{2,0,1:T(4,128)(2,1)} %copy.68), calls=%async_computation.3 | async-start | bytes 9437184 | tf_op jit(solution)/shard_map/all_to_all | solution.py:26
  91.4 8.1 %add_convert_fusion.2 = bf16[3,1024,384]{2,1,0:T(8,128)(2,1)S(1)} fusion(bf16[3,1024,384]{2,1,0:T(8,128)(2,1)S(1)} %convolution_convert_fusion, bf16[3,1024,1536]{2,1,0:T(8,128)(2,1)} %copy-done.4, bf16[4,384,1536]{2,1,0:T(8,128)(2,1)} %param.7), kind=kOutput, calls=%fused_computation.78 | convolution fusion | flops 3627417600 | bytes 15335424 | tf_op jit(solution)/shard_map/tbf,df->tbd/dot_general | solution.py:59
  100.9 8.7 %fusion.51 = bf16[3,1536,384]{1,2,0:T(8,128)(2,1)} fusion(bf16[3,1024,384]{2,1,0:T(8,128)(2,1)S(1)} %add_convert_fusion.2, f32[1024,1536]{1,0:T(8,128)} %copy-done.15), kind=kOutput, calls=%fused_computation.85 | convolution fusion | flops 3641573376 | bytes 12189696 | tf_op jit(solution)/shard_map/bf,tbd->tfd/dot_general | solution.py:52
  115.6 7.3 convert_element_type.238
  122.9 7.1 copy.77
  130.1 28.2 %all-to-all-done.3 = bf16[3,128,4608]{2,0,1:T(4,128)(2,1)} async-done(((bf16[3,128,4608]{2,0,1:T(4,128)(2,1)}), bf16[3,128,4608]{2,0,1:T(4,128)(2,1)}, u32[]{:S(2)}, u32[]{:S(2)}) %all-to-all-start.3) | async-done | bytes 3538976 | tf_op jit(solution)/shard_map/all_to_all | solution.py:26
  158.2 7.2 all-to-all-start.6
  165.4 8.2 %multiply_convert_fusion.2 = bf16[3,1024,1536]{2,1,0:T(8,128)(2,1)S(1)} fusion(f32[1024,1536]{1,0:T(8,128)} %get-tuple-element.58, bf16[3,1024,384]{2,1,0:T(8,128)(2,1)} %copy-done.7, bf16[4,1536,384]{2,1,0:T(8,128)(2,1)} %param.8), kind=kOutput, calls=%fused_computation.3 | convolution fusion | flops 3633315840 | bytes 19267584 | tf_op jit(solution)/shard_map/tbd,fd->tbf/dot_general | solution.py:54
  177.3 6.6 fusion.47
  196.1 7.1 copy.65
  203.3 29.0 %all-to-all-done.6 = bf16[3,128,4608]{2,0,1:T(4,128)(2,1)} async-done(((bf16[3,128,4608]{2,0,1:T(4,128)(2,1)}), bf16[3,128,4608]{2,0,1:T(4,128)(2,1)}, u32[]{:S(2)}, u32[]{:S(2)}) %all-to-all-start.6) | async-done | bytes 3538976 | tf_op jit(solution)/shard_map/all_to_all | solution.py:26
  232.3 7.4 all-to-all-start.2
  239.7 8.4 %add_convert_fusion.1 = bf16[3,1024,384]{2,1,0:T(8,128)(2,1)S(1)} fusion(bf16[3,1024,384]{2,1,0:T(8,128)(2,1)} %copy-done.7, bf16[3,1024,1536]{2,1,0:T(8,128)(2,1)} %copy-done.2, bf16[4,384,1536]{2,1,0:T(8,128)(2,1)} %param.7), kind=kOutput, calls=%fused_computation.77 | convolution fusion | flops 3627417600 | bytes 15335424 | tf_op jit(solution)/shard_map/tbf,df->tbd/dot_general | solution.py:59
  249.5 8.7 %fusion.50 = bf16[3,1536,384]{1,2,0:T(8,128)(2,1)} fusion(bf16[3,1024,384]{2,1,0:T(8,128)(2,1)S(1)} %add_convert_fusion.1, f32[1024,1536]{1,0:T(8,128)} %copy-done.14), kind=kOutput, calls=%fused_computation.84 | convolution fusion | flops 3641573376 | bytes 12189696 | tf_op jit(solution)/shard_map/bf,tbd->tfd/dot_general | solution.py:52
  264.2 7.3 convert_element_type.234
  271.5 7.1 copy.74
  278.7 27.9 %all-to-all-done.2 = bf16[3,128,4608]{2,0,1:T(4,128)(2,1)} async-done(((bf16[3,128,4608]{2,0,1:T(4,128)(2,1)}), bf16[3,128,4608]{2,0,1:T(4,128)(2,1)}, u32[]{:S(2)}, u32[]{:S(2)}) %all-to-all-start.2) | async-done | bytes 3538976 | tf_op jit(solution)/shard_map/all_to_all | solution.py:26
  306.5 7.1 all-to-all-start.5
  313.7 8.2 %multiply_convert_fusion.1 = bf16[3,1024,1536]{2,1,0:T(8,128)(2,1)S(1)} fusion(f32[1024,1536]{1,0:T(8,128)} %get-tuple-element.60, bf16[3,1024,384]{2,1,0:T(8,128)(2,1)} %copy-done.6, bf16[4,1536,384]{2,1,0:T(8,128)(2,1)} %param.8), kind=kOutput, calls=%fused_computation.2 | convolution fusion | flops 3633315840 | bytes 19267584 | tf_op jit(solution)/shard_map/tbd,fd->tbf/dot_general | solution.py:54
  325.6 6.6 fusion.46
  338.3 6.2 convert_element_type.218
  344.4 7.1 copy.62
  351.6 29.0 %all-to-all-done.5 = bf16[3,128,4608]{2,0,1:T(4,128)(2,1)} async-done(((bf16[3,128,4608]{2,0,1:T(4,128)(2,1)}), bf16[3,128,4608]{2,0,1:T(4,128)(2,1)}, u32[]{:S(2)}, u32[]{:S(2)}) %all-to-all-start.5) | async-done | bytes 3538976 | tf_op jit(solution)/shard_map/all_to_all | solution.py:26
  380.5 7.2 all-to-all-start.1
  387.7 9.5 %add_convert_fusion = bf16[3,1024,384]{2,1,0:T(8,128)(2,1)} fusion(bf16[3,1024,384]{2,1,0:T(8,128)(2,1)} %copy-done.6, bf16[3,1024,1536]{2,1,0:T(8,128)(2,1)} %copy-done.3, bf16[4,384,1536]{2,1,0:T(8,128)(2,1)} %param.7), kind=kOutput, calls=%fused_computation.76 | convolution fusion | flops 3627417600 | bytes 15335424 | tf_op jit(solution)/shard_map/tbf,df->tbd/dot_general | solution.py:59
  397.2 23.1 %fusion.45 = bf16[3,384,1536]{1,2,0:T(8,128)(2,1)} fusion(f32[1024,1536]{1,0:T(8,128)} %get-tuple-element.54, bf16[3,1024,384]{2,1,0:T(8,128)(2,1)} %add_convert_fusion, bf16[4,1536,384]{2,1,0:T(8,128)(2,1)} %param.8, bf16[1024,384]{1,0:T(8,128)(2,1)S(1)} %copy-done.12), kind=kOutput, calls=%fused_computation.79 | convolution fusion | flops 7260733440 | bytes 14155776 | tf_op jit(solution)/shard_map/bd,tbf->tdf/dot_general | solution.py:56
  426.4 6.5 convert_element_type.214
  432.9 7.2 copy.59
  440.1 14.5 %all-to-all-done.1 = bf16[3,128,4608]{2,0,1:T(4,128)(2,1)} async-done(((bf16[3,128,4608]{2,0,1:T(4,128)(2,1)}), bf16[3,128,4608]{2,0,1:T(4,128)(2,1)}, u32[]{:S(2)}, u32[]{:S(2)}) %all-to-all-start.1) | async-done | bytes 3538976 | tf_op jit(solution)/shard_map/all_to_all | solution.py:26
  454.6 6.8 all-to-all-start
  461.4 9.3 %fusion.49 = bf16[3,1536,384]{1,2,0:T(8,128)(2,1)} fusion(bf16[3,1024,384]{2,1,0:T(8,128)(2,1)} %add_convert_fusion, f32[1024,1536]{1,0:T(8,128)} %copy-done.13), kind=kOutput, calls=%fused_computation.83 | convolution fusion | flops 3641573376 | bytes 12189696 | tf_op jit(solution)/shard_map/bf,tbd->tfd/dot_general | solution.py:52
  476.8 7.3 convert_element_type.230
  484.0 7.2 copy.71
  491.2 36.5 %all-to-all-done = bf16[3,128,4608]{2,0,1:T(4,128)(2,1)} async-done(((bf16[3,128,4608]{2,0,1:T(4,128)(2,1)}), bf16[3,128,4608]{2,0,1:T(4,128)(2,1)}, u32[]{:S(2)}, u32[]{:S(2)}) %all-to-all-start) | async-done | bytes 3538976 | tf_op jit(solution)/shard_map/all_to_all | solution.py:26
  527.7 10.2 %all-to-all-start.4 = ((bf16[3,128,4608]{2,0,1:T(4,128)(2,1)}), bf16[3,128,4608]{2,0,1:T(4,128)(2,1)}, u32[]{:S(2)}, u32[]{:S(2)}) async-start(bf16[3,128,4608]{2,0,1:T(4,128)(2,1)} %copy.71), calls=%async_computation.4 | async-start | bytes 9437184 | tf_op jit(solution)/shard_map/all_to_all | solution.py:26
  537.9 8.7 %fusion.52 = bf16[3,1536,384]{1,2,0:T(8,128)(2,1)} fusion(bf16[3,1024,384]{2,1,0:T(8,128)(2,1)S(1)} %convolution_convert_fusion, f32[1024,1536]{1,0:T(8,128)} %get-tuple-element.57), kind=kOutput, calls=%fused_computation.86 | convolution fusion | flops 3641573376 | bytes 12189696 | tf_op jit(solution)/shard_map/bf,tbd->tfd/dot_general | solution.py:52
  552.6 7.5 convert_element_type.242
  560.1 7.2 copy.80
  576.2 28.6 %all-to-all-done.4 = bf16[3,128,4608]{2,0,1:T(4,128)(2,1)} async-done(((bf16[3,128,4608]{2,0,1:T(4,128)(2,1)}), bf16[3,128,4608]{2,0,1:T(4,128)(2,1)}, u32[]{:S(2)}, u32[]{:S(2)}) %all-to-all-start.4) | async-done | bytes 3538976 | tf_op jit(solution)/shard_map/all_to_all | solution.py:26
  604.8 7.0 all-to-all-start.7
  635.6 42.2 %all-to-all-done.7 = bf16[3,128,4608]{2,0,1:T(4,128)(2,1)} async-done(((bf16[3,128,4608]{2,0,1:T(4,128)(2,1)}), bf16[3,128,4608]{2,0,1:T(4,128)(2,1)}, u32[]{:S(2)}, u32[]{:S(2)}) %all-to-all-start.7) | async-done | bytes 3538976 | tf_op jit(solution)/shard_map/all_to_all | solution.py:26
  682.8 67.0 %psum.7 = f32[3,3]{1,0:T(4,128)S(1)} all-reduce(f32[3,3]{1,0:T(4,128)S(1)} %convolution_add_fusion), channel_id=1, replica_groups=mesh['data'=128] {'data'}, use_global_device_ids=true, to_apply=%region_10.0 | all-reduce | flops 9 | bytes 72 | tf_op jit(solution)/shard_map/psum | solution.py:61
  (148 shorter events, 173.6 us)
Async XLA Ops:
  0.6 34.9 %copy-start = (bf16[3,384,13]{1,2,0:T(8,128)(2,1)S(1)}, bf16[3,384,13]{1,2,0:T(8,128)(2,1)}, u32[]{:S(2)}) copy-start(bf16[3,384,13]{1,2,0:T(8,128)(2,1)} %param.9) | copy-start | bytes 89860
  0.6 8.6 %copy-start.11 = (bf16[1024,384]{1,0:T(8,128)(2,1)S(1)}, bf16[1024,384]{1,0:T(8,128)(2,1)}, u32[]{:S(2)}) copy-start(bf16[1024,384]{1,0:T(8,128)(2,1)} %param.5) | copy-start | bytes 2359300
  0.7 8.6 %copy-start.5 = (bf16[4,1536,384]{2,1,0:T(8,128)(2,1)S(1)}, bf16[4,1536,384]{2,1,0:T(8,128)(2,1)}, u32[]{:S(2)}) copy-start(bf16[4,1536,384]{2,1,0:T(8,128)(2,1)} %param.8) | copy-start | bytes 14155780
  0.7 11.2 %slice-start = ((s8[4718592]{0:T(1024)(128)(4,1)}), s8[4194304]{0:T(1024)(128)(4,1)S(1)}, s32[]{:S(2)}) async-start(s8[4718592]{0:T(1024)(128)(4,1)} %bitcast.143), calls=%async_computation.8 | async-start | bytes 8388608
  9.2 2.6 copy-start.13
  9.2 2.6 slice-start.1
  11.8 6.0 copy-start.16
  17.8 2.6 copy-start.14
  20.4 5.8 copy-start.18
  26.2 2.6 copy-start.15
  35.5 5.5 copy-start.9
  49.5 3.6 copy-start.4
  79.1 79.1 %all-to-all-start.3 = ((bf16[3,128,4608]{2,0,1:T(4,128)(2,1)}), bf16[3,128,4608]{2,0,1:T(4,128)(2,1)}, u32[]{:S(2)}, u32[]{:S(2)}) async-start(bf16[3,128,4608]{2,0,1:T(4,128)(2,1)} %copy.68), calls=%async_computation.3 | async-start | bytes 9437184 | tf_op jit(solution)/shard_map/all_to_all | solution.py:26
  99.5 1.4 copy-start.7
  158.2 74.0 %all-to-all-start.6 = ((bf16[3,128,4608]{2,0,1:T(4,128)(2,1)}), bf16[3,128,4608]{2,0,1:T(4,128)(2,1)}, u32[]{:S(2)}, u32[]{:S(2)}) async-start(bf16[3,128,4608]{2,0,1:T(4,128)(2,1)} %copy.77), calls=%async_computation.6 | async-start | bytes 9437184 | tf_op jit(solution)/shard_map/all_to_all | solution.py:26
  165.4 11.9 %copy-start.19 = (bf16[1024,384]{1,0:T(8,128)(2,1)S(1)}, bf16[1024,384]{1,0:T(8,128)(2,1)}, u32[]{:S(2)}) copy-start(bf16[1024,384]{1,0:T(8,128)(2,1)} %copy-done.18) | copy-start | bytes 2359300
  173.7 3.6 copy-start.2
  232.3 74.2 %all-to-all-start.2 = ((bf16[3,128,4608]{2,0,1:T(4,128)(2,1)}), bf16[3,128,4608]{2,0,1:T(4,128)(2,1)}, u32[]{:S(2)}, u32[]{:S(2)}) async-start(bf16[3,128,4608]{2,0,1:T(4,128)(2,1)} %copy.65), calls=%async_computation.2 | async-start | bytes 9437184 | tf_op jit(solution)/shard_map/all_to_all | solution.py:26
  248.1 1.4 copy-start.6
  306.5 74.0 %all-to-all-start.5 = ((bf16[3,128,4608]{2,0,1:T(4,128)(2,1)}), bf16[3,128,4608]{2,0,1:T(4,128)(2,1)}, u32[]{:S(2)}, u32[]{:S(2)}) async-start(bf16[3,128,4608]{2,0,1:T(4,128)(2,1)} %copy.74), calls=%async_computation.5 | async-start | bytes 9437184 | tf_op jit(solution)/shard_map/all_to_all | solution.py:26
  313.7 11.9 %copy-start.17 = (bf16[1024,384]{1,0:T(8,128)(2,1)S(1)}, bf16[1024,384]{1,0:T(8,128)(2,1)}, u32[]{:S(2)}) copy-start(bf16[1024,384]{1,0:T(8,128)(2,1)} %copy-done.16) | copy-start | bytes 2359300
  321.9 3.6 copy-start.3
  380.5 74.0 %all-to-all-start.1 = ((bf16[3,128,4608]{2,0,1:T(4,128)(2,1)}), bf16[3,128,4608]{2,0,1:T(4,128)(2,1)}, u32[]{:S(2)}, u32[]{:S(2)}) async-start(bf16[3,128,4608]{2,0,1:T(4,128)(2,1)} %copy.62), calls=%async_computation.1 | async-start | bytes 9437184 | tf_op jit(solution)/shard_map/all_to_all | solution.py:26
  387.7 9.5 %copy-start.12 = (bf16[1024,384]{1,0:T(8,128)(2,1)S(1)}, bf16[1024,384]{1,0:T(8,128)(2,1)}, u32[]{:S(2)}) copy-start(bf16[1024,384]{1,0:T(8,128)(2,1)} %param.5) | copy-start | bytes 2359300
  454.6 73.1 %all-to-all-start = ((bf16[3,128,4608]{2,0,1:T(4,128)(2,1)}), bf16[3,128,4608]{2,0,1:T(4,128)(2,1)}, u32[]{:S(2)}, u32[]{:S(2)}) async-start(bf16[3,128,4608]{2,0,1:T(4,128)(2,1)} %copy.59), calls=%async_computation | async-start | bytes 9437184 | tf_op jit(solution)/shard_map/all_to_all | solution.py:26
  527.7 77.1 %all-to-all-start.4 = ((bf16[3,128,4608]{2,0,1:T(4,128)(2,1)}), bf16[3,128,4608]{2,0,1:T(4,128)(2,1)}, u32[]{:S(2)}, u32[]{:S(2)}) async-start(bf16[3,128,4608]{2,0,1:T(4,128)(2,1)} %copy.71), calls=%async_computation.4 | async-start | bytes 9437184 | tf_op jit(solution)/shard_map/all_to_all | solution.py:26
  604.8 73.1 %all-to-all-start.7 = ((bf16[3,128,4608]{2,0,1:T(4,128)(2,1)}), bf16[3,128,4608]{2,0,1:T(4,128)(2,1)}, u32[]{:S(2)}, u32[]{:S(2)}) async-start(bf16[3,128,4608]{2,0,1:T(4,128)(2,1)} %copy.80), calls=%async_computation.7 | async-start | bytes 9437184 | tf_op jit(solution)/shard_map/all_to_all | solution.py:26
  626.3 166.1 %copy-start.1 = (bf16[3,384,13]{1,2,0:T(8,128)(2,1)S(1)}, bf16[3,384,13]{1,2,0:T(8,128)(2,1)}, u32[]{:S(2)}) copy-start(bf16[3,384,13]{1,2,0:T(8,128)(2,1)} %param.9) | copy-start | bytes 89860
  749.8 42.6 %copy-start.8 = (f32[3,3]{1,0:T(4,128)}, f32[3,3]{1,0:T(4,128)S(1)}, u32[]{:S(2)}) copy-start(f32[3,3]{1,0:T(4,128)S(1)} %psum.7) | copy-start | bytes 112
  790.9 1.4 copy-start.10
where the time goes:
time: 802 us; the launch traced here: 793 us
  waiting for transfers between devices  236 us (29%)
  local copies, waits for them, and re-layouts  175 us (22%)
  matrix products  172 us (21%)
  other arithmetic  75.9 us (9%)
  blocking collectives  67 us (8%)
  starting transfers between devices  65.1 us (8%)
    all_to_all x8, waiting for transfers between devices, scatter_sum(): received = lax.all_to_all(flat_part, 'data', 1, 0, tiled=True)  236 us
    convert_element_type x24, local copies, waits for them, and re-layouts, scatter_sum(): (part_grad.reshape(num_tasks, -1) * inv_tokens).astype(jnp.bfloat16)  160 us
    psum x1, blocking collectives, local_step(): gram_mat = lax.psum(gram_part, 'data')  67 us
    all_to_all x8, starting transfers between devices, scatter_sum(): received = lax.all_to_all(flat_part, 'data', 1, 0, tiled=True)  65.1 us
    dot_general x4, matrix products, local_step(): jnp.einsum('bd,tbf->tdf', hidden_in, d_pre, preferred_element_type=jnp.fl...  42.9 us
    dot_general x4, matrix products, local_step(): jnp.einsum('bf,tbd->tfd', act_bf, d_hidden, preferred_element_type=jnp.fl...  35.3 us
    reduce_sum x8, other arithmetic, scatter_sum(): return jnp.sum(received, axis=0, dtype=jnp.float32)  34.3 us
    dot_general x4, matrix products, local_step(): jnp.dot(hidden, w_up[layer_idx], preferred_element_type=jnp.float32)  27 us
  transfers between devices with their start and end apart: 8, of which 8 were waited for; matrix products, arithmetic and copies ran while one was open for 36% of the time, Pallas kernels for 0%

commit v1 on v0

v1 whole, which is shorter than its diff:
```python
import functools

import jax
import jax.numpy as jnp
from jax import lax
from jax.experimental import pallas as pl
from jax.experimental.pallas import tpu as pltpu
from jax.sharding import PartitionSpec as P

EG_STEPS = 20
NT = 3
NL = 4
DM = 384
DF = 1536
TOK = 1024
UNITS = NT * NL
AXIS_STRIDE = (2, 8, 32)
MESH = pl.DeviceIdType.MESH
F32 = jnp.float32
BF16 = jnp.bfloat16


def simplex_weights(gram_mat):
    num_tasks = gram_mat.shape[0]
    value_a11 = jnp.trace(gram_mat) / num_tasks
    alpha_vec = jnp.full((num_tasks,), 1.0 / num_tasks, jnp.float32)
    for step_idx in range(EG_STEPS):
        grad_pull = jnp.sum(gram_mat * alpha_vec[None, :], axis=1)
        alpha_vec = alpha_vec * jnp.exp(-grad_pull / value_a11)
        alpha_vec = alpha_vec / jnp.sum(alpha_vec)
    return alpha_vec


def half_slice(half):
    return slice(None) if half is None else pl.ds(2 * half, 2)


def backward_kernel(*refs):
    (at0, at1, at2, at3, ht0, ht1, ht2, ht3, sl0, sl1, sl2, sl3,
     w1t_hbm, w2t_hbm, d0_hbm, out_ref,
     at, ht, sl, w1t, w2t, dbuf, sbuf, tmp,
     gown, gsend, rd2d, ra1, rb1, acc2, ra2, rb2, acc3, r3,
     load_sem, d_sem, d2d_s, d2d_r, a1_s, a1_r, b1_s, b1_r,
     a2_s, a2_r, b2_s, b2_r, c3_s, c3_r) = refs
    at_hbm, ht_hbm, sl_hbm = (at0, at1, at2, at3), (ht0, ht1, ht2, ht3), (sl0, sl1, sl2, sl3)

    me = lax.axis_index('data')
    core = lax.rem(me, 2)
    pos = [lax.rem(me // s, 4) for s in AXIS_STRIDE]
    sibling = me + 1 - 2 * core

    def at_pos(axis, k):
        return lax.rem(pos[axis] + k, 4)

    def peer(axis, k):
        return me + (at_pos(axis, k) - pos[axis]) * AXIS_STRIDE[axis]

    barrier = pltpu.get_barrier_semaphore()
    partners = [sibling] + [peer(a, k) for a in range(3) for k in (1, 2, 3)]
    for dev in partners:
        pl.semaphore_signal(barrier, inc=1, device_id=(dev,), device_id_type=MESH)

    def loads(layer, slot):
        return [
            pltpu.make_async_copy(at_hbm[layer], at.at[slot], load_sem.at[0, slot]),
            pltpu.make_async_copy(ht_hbm[layer], ht.at[slot], load_sem.at[1, slot]),
            pltpu.make_async_copy(sl_hbm[layer], sl.at[slot], load_sem.at[2, slot]),
            pltpu.make_async_copy(w1t_hbm.at[layer], w1t.at[slot], load_sem.at[3, slot]),
            pltpu.make_async_copy(w2t_hbm.at[layer], w2t.at[slot], load_sem.at[4, slot]),
        ]

    d_load = pltpu.make_async_copy(d0_hbm, dbuf, d_sem)
    d_load.start()
    for cp in loads(NL - 1, 0):
        cp.start()
    pl.semaphore_wait(barrier, len(partners))
    d_load.wait()

    def remote(src, dst, send, recv, dev):
        return pltpu.make_async_remote_copy(
            src_ref=src, dst_ref=dst, send_sem=send, recv_sem=recv,
            device_id=(dev,), device_id_type=MESH)

    def chunk1(g3, p, idx, half=None):
        h, rows = half_slice(half), pl.ds(24 * p, 24)
        return (gown.at[g3, h, :, idx, rows, :], gown.at[g3, h, idx, :, rows, :],
                gown.at[g3, idx, h, :, rows, :])[p]

    def chunk2(par, p, idx, half=None):
        h = half_slice(half)
        return (acc2.at[par, 0, h, idx], acc2.at[par, 1, idx, h], acc2.at[par, 2, h, idx])[p]

    def d2d_copies(v):
        par = lax.rem(v, 2)
        return [remote(gsend.at[par], rd2d.at[par], d2d_s.at[par], d2d_r.at[par], sibling)]

    def relay1(v):
        par, g3 = lax.rem(v, 2), lax.rem(v, 3)
        return [remote(chunk1(g3, p, at_pos(p, 2), d), ra1.at[par, p, d], a1_s.at[par, p, d],
                       a1_r.at[par, p, d], peer(p, 1 + 2 * d)) for p in range(3) for d in range(2)]

    def main1(v):
        par, g3 = lax.rem(v, 2), lax.rem(v, 3)
        return [remote(chunk1(g3, p, at_pos(p, 1 + 2 * d)), rb1.at[par, p, d], b1_s.at[par, p, d],
                       b1_r.at[par, p, d], peer(p, 1 + 2 * d)) for p in range(3) for d in range(2)]

    def relay2(v):
        par = lax.rem(v, 2)
        return [remote(chunk2(par, p, at_pos((p + 1) % 3, 2), d), ra2.at[par, p, d], a2_s.at[par, p, d],
                       a2_r.at[par, p, d], peer((p + 1) % 3, 1 + 2 * d)) for p in range(3) for d in range(2)]

    def main2(v):
        par = lax.rem(v, 2)
        return [remote(chunk2(par, p, at_pos((p + 1) % 3, 1 + 2 * d)), rb2.at[par, p, d], b2_s.at[par, p, d],
                       b2_r.at[par, p, d], peer((p + 1) % 3, 1 + 2 * d)) for p in range(3) for d in range(2)]

    def last3(v):
        par = lax.rem(v, 2)
        return [remote(acc3.at[par, p, at_pos((p + 2) % 3, k)], r3.at[par, p, k - 1], c3_s.at[par, p, k - 1],
                       c3_r.at[par, p, k - 1], peer((p + 2) % 3, k)) for p in range(3) for k in (1, 2, 3)]

    def start(copies):
        for cp in copies:
            cp.start()

    def wait(copies):
        for cp in copies:
            cp.wait()

    def step_d2d(v):
        wait(d2d_copies(v))
        par, g3 = lax.rem(v, 2), lax.rem(v, 3)

        def add(i, carry):
            gown[g3, i] = gown[g3, i] + rd2d[par, i]
            return carry

        lax.fori_loop(0, 4, add, 0)
        start(relay1(v))

    def step_relay1(v):
        wait(relay1(v))
        par, g3 = lax.rem(v, 2), lax.rem(v, 3)
        for p in range(3):
            for d in range(2):
                dst = chunk1(g3, p, at_pos(p, 1 + 2 * d), d)
                dst[...] = dst[...] + ra1[par, p, d]
        start(main1(v))

    def step_main1(v):
        wait(main1(v))
        par, g3 = lax.rem(v, 2), lax.rem(v, 3)
        for p in range(3):
            acc2[par, p] = chunk1(g3, p, pos[p])[...] + rb1[par, p, 0] + rb1[par, p, 1]
        start(relay2(v))

    def step_relay2(v):
        wait(relay2(v))
        par = lax.rem(v, 2)
        for p in range(3):
            for d in range(2):
                dst = chunk2(par, p, at_pos((p + 1) % 3, 1 + 2 * d), d)
                dst[...] = dst[...] + ra2[par, p, d]
        start(main2(v))

    def step_main2(v):
        wait(main2(v))
        par = lax.rem(v, 2)
        for p in range(3):
            acc3[par, p] = chunk2(par, p, pos[(p + 1) % 3])[...] + rb2[par, p, 0] + rb2[par, p, 1]
        start(last3(v))

    def step_last3(v):
        wait(last3(v))
        par = lax.rem(v, 2)
        for p in range(3):
            out_ref[v, pl.ds(24 * p, 24), :] = (
                (acc3[par, p, pos[(p + 2) % 3]] + r3[par, p, 0]) + (r3[par, p, 1] + r3[par, p, 2]))

    def when_unit(v, step):
        pl.when(jnp.logical_and(v >= 0, v < UNITS))(lambda: step(v))

    def body(u, carry):
        li, task = u // NT, lax.rem(u, NT)
        slot = lax.rem(li, 2)
        par, g3 = lax.rem(u, 2), lax.rem(u, 3)
        computing = u < UNITS

        def dest(rel):
            if rel == 0:
                return gown.at[g3].reshape(64 * 72, 128)
            return gsend.at[par].reshape(64 * 72, 128)

        for k in range(NL):
            @pl.when(jnp.logical_and(task == 0, li == k))
            def _(k=k):
                for cp in loads(NL - 1 - k, k % 2):
                    cp.wait()
                if k + 1 < NL:
                    for cp in loads(NL - 2 - k, (k + 1) % 2):
                        cp.start()

        @pl.when(computing)
        def _():
            for m in range(4):
                val = jnp.dot(at[slot, 384 * m:384 * (m + 1), :], dbuf[task], preferred_element_type=F32)
                for lb in range(3):
                    tmp[m % 2, lb] = val[:, 128 * lb:128 * (lb + 1)]
                for rel in range(2):
                    cc = core if rel == 0 else 1 - core
                    dst = dest(rel)
                    for j in range(12):
                        for lb in range(3):
                            dst[pl.ds(m * 16 * 72 + 36 + 3 * j + lb, 16, stride=72), :] = (
                                tmp[m % 2, lb, pl.ds(12 * cc + j, 16, stride=24), :])

        when_unit(u - 3, step_relay2)
        when_unit(u - 4, step_last3)

        @pl.when(computing)
        def _():
            def block(mb, c):
                rows = pl.ds(pl.multiple_of(mb * 512, 512), 512)
                for n in range(6):
                    cols = slice(256 * n, 256 * (n + 1))
                    val = jnp.dot(dbuf[task, rows, :], w2t[slot, :, cols], preferred_element_type=F32)
                    sbuf[rows, cols] = (val * sl[slot, rows, cols]).astype(BF16)
                return c
            lax.fori_loop(0, 2, block, 0)

        when_unit(u - 1, step_d2d)

        @pl.when(computing)
        def _():
            for n in range(6):
                val = jnp.dot(ht[slot], sbuf[:, 256 * n:256 * (n + 1)], preferred_element_type=F32)
                for lb in range(2):
                    tmp[n % 2, lb] = val[:, 128 * lb:128 * (lb + 1)]
                for rel in range(2):
                    cc = core if rel == 0 else 1 - core
                    dst = dest(rel)
                    for r in range(3):
                        for lb in range(2):
                            dst[pl.ds(12 * r + 2 * n + lb, 64, stride=72), :] = (
                                tmp[n % 2, lb, pl.ds(3 * cc + r, 64, stride=6), :])

        when_unit(u, lambda v: start(d2d_copies(v)))
        when_unit(u - 3, step_main2)
        when_unit(u - 2, step_main1)

        @pl.when(u < UNITS - NT)
        def _():
            def block(mb, c):
                rows = pl.ds(pl.multiple_of(mb * 512, 512), 512)
                val = jnp.dot(sbuf[rows, :], w1t[slot], preferred_element_type=F32)
                dbuf[task, rows, :] = (dbuf[task, rows, :].astype(F32) + val).astype(BF16)
                return c
            lax.fori_loop(0, 2, block, 0)

        when_unit(u - 1, step_relay1)
        return carry

    lax.fori_loop(0, UNITS + 4, body, 0)


def backward(acts_t, hid_t, slopes, w1t, w2t, d0):
    any_spec = pl.BlockSpec(memory_space=pl.ANY)
    dma = pltpu.SemaphoreType.DMA
    scratch = [
        pltpu.VMEM((2, DF, TOK), BF16),
        pltpu.VMEM((2, DM, TOK), BF16),
        pltpu.VMEM((2, TOK, DF), F32),
        pltpu.VMEM((2, DF, DM), BF16),
        pltpu.VMEM((2, DM, DF), BF16),
        pltpu.VMEM((NT, TOK, DM), BF16),
        pltpu.VMEM((TOK, DF), BF16),
        pltpu.VMEM((2, 3, 384, 128), F32),
        pltpu.VMEM((3, 4, 4, 4, 72, 128), F32),
        pltpu.VMEM((2, 4, 4, 4, 72, 128), F32),
        pltpu.VMEM((2, 4, 4, 4, 72, 128), F32),
        pltpu.VMEM((2, 3, 2, 2, 4, 24, 128), F32),
        pltpu.VMEM((2, 3, 2, 4, 4, 24, 128), F32),
        pltpu.VMEM((2, 3, 4, 4, 24, 128), F32),
        pltpu.VMEM((2, 3, 2, 2, 24, 128), F32),
        pltpu.VMEM((2, 3, 2, 4, 24, 128), F32),
        pltpu.VMEM((2, 3, 4, 24, 128), F32),
        pltpu.VMEM((2, 3, 3, 24, 128), F32),
        dma((5, 2)), dma, dma((2,)), dma((2,)),
        dma((2, 3, 2)), dma((2, 3, 2)), dma((2, 3, 2)), dma((2, 3, 2)),
        dma((2, 3, 2)), dma((2, 3, 2)), dma((2, 3, 2)), dma((2, 3, 2)),
        dma((2, 3, 3)), dma((2, 3, 3)),
    ]
    return pl.pallas_call(
        backward_kernel,
        out_shape=jax.ShapeDtypeStruct((UNITS, 72, 128), F32),
        in_specs=[any_spec] * 15,
        out_specs=pl.BlockSpec(memory_space=pltpu.VMEM),
        scratch_shapes=scratch,
        compiler_params=pltpu.CompilerParams(
            collective_id=0, has_side_effects=True, vmem_limit_bytes=67043328),
        cost_estimate=pl.CostEstimate(flops=58 * 10**9, bytes_accessed=60 * 10**6, transcendentals=0),
    )(*acts_t, *hid_t, *slopes, w1t, w2t, d0)


def solution(mesh):
    num_dev = mesh.shape['data']

    def local_step(x_local, lab_local, w_up, w_down, task_heads):
        num_layers = w_up.shape[0]
        num_classes = task_heads.shape[2]
        inv_tokens = 1.0 / (x_local.shape[0] * num_dev)
        hidden = x_local
        acts_t, hid_t, slopes = [], [], []
        for layer_idx in range(num_layers):
            pre_act = jnp.dot(hidden, w_up[layer_idx], preferred_element_type=F32)
            act_val, gelu_slope = jax.jvp(jax.nn.gelu, (pre_act,), (jnp.ones_like(pre_act),))
            act_bf = act_val.astype(BF16)
            mlp_out = jnp.dot(act_bf, w_down[layer_idx], preferred_element_type=F32)
            acts_t.append(act_bf.T)
            hid_t.append(hidden.T)
            slopes.append(gelu_slope)
            hidden = (hidden.astype(F32) + mlp_out).astype(BF16)
        logits = jnp.einsum('bd,tdc->tbc', hidden, task_heads, preferred_element_type=F32)
        soft_probs = jax.nn.softmax(logits, axis=-1)
        onehot = (lab_local[:, :, None] == jnp.arange(num_classes)[None, None, :]).astype(F32)
        head_err = (soft_probs - onehot).astype(BF16)
        d_hidden = jnp.einsum('tbc,tdc->tbd', head_err, task_heads, preferred_element_type=F32).astype(BF16)
        shares = backward(acts_t, hid_t, slopes, jnp.swapaxes(w_up, 1, 2), jnp.swapaxes(w_down, 1, 2), d_hidden)
        shares = shares.reshape(num_layers, NT, 72 * 128)[::-1] * inv_tokens
        gram_part = jnp.sum(shares[:, :, None, :] * shares[:, None, :, :], axis=(0, 3))
        gram_mat = lax.psum(gram_part, 'data')
        task_weights = simplex_weights(gram_mat)
        mixed = jnp.sum(task_weights[None, :, None] * shares, axis=1)
        return task_weights, gram_mat, mixed[:, :36 * 128], mixed[:, 36 * 128:]

    return jax.shard_map(local_step, mesh=mesh, in_specs=(P('data', None), P(None, 'data'), P(), P(), P()), out_specs=(P(), P(), P(None, 'data'), P(None, 'data')), check_vma=False)
```

time: 802 us -> 386 us (0.48)
  waiting for transfers between devices: 236 us -> 0 us
  Pallas kernels: 0 us -> 149 us
  local copies, waits for them, and re-layouts: 175 us -> 45 us
  matrix products: 172 us -> 60.4 us
  starting transfers between devices: 65.1 us -> 0 us
  other arithmetic: 75.9 us -> 58.5 us
    all_to_all x8 -> x0, waiting for transfers between devices: 236 us -> none  [scatter_sum(): received = lax.all_to_all(flat_part, 'data', 1, 0, tiled=True)]
    convert_element_type x24 -> x0, local copies, waits for them, and re-layouts: 160 us -> none  [scatter_sum(): (part_grad.reshape(num_tasks, -1) * inv_tokens).astype(jnp.bfloat16)]
    pallas_call x0 -> x1, Pallas kernels: none -> 149 us  [backward(): pl.pallas_call(backward_kernel, out_shape=jax.ShapeDtypeStruct((UNITS, 72...]
    dot_general x31 -> x9, matrix products: 172 us -> 60.4 us  [the longest x4 37 us: local_step(): pre_act = jnp.dot(hidden, w_up[layer_idx], preferred_element_type=F32)]
    all_to_all x8 -> x0, starting transfers between devices: 65.1 us -> none  [scatter_sum(): received = lax.all_to_all(flat_part, 'data', 1, 0, tiled=True)]
    reduce_sum x9 -> x2, other arithmetic: 34.7 us -> 0.54 us  [the longest x1 0.37 us: local_step(): jnp.sum(shares[:, :, None, :] * shares[:, None, :, :], axis=(0, 3))]
    dot_general x0 -> x4, local copies, waits for them, and re-layouts: none -> 26.9 us  [local_step(): pre_act = jnp.dot(hidden, w_up[layer_idx], preferred_element_type=F32)]
    convert_element_type x0 -> x2, other arithmetic: none -> 16.9 us  [local_step(): act_bf = act_val.astype(BF16)]
  transfers between devices with their start and end apart: 8 -> 0, of which waited for: 8 -> 0; matrix products, arithmetic and copies ran while one was open for 36% -> 0% of each run, Pallas kernels for 0% -> 0%
where the time goes in v1:
time: 386 us; the launch traced here: 381 us
  Pallas kernels  149 us (39%)
  blocking collectives  66.8 us (17%)
  matrix products  60.4 us (16%)
  other arithmetic  58.5 us (15%)
  local copies, waits for them, and re-layouts  45 us (12%)
    pallas_call x1, Pallas kernels, backward(): pl.pallas_call(backward_kernel, out_shape=jax.ShapeDtypeStruct((UNITS, 72...  149 us
    psum x1, blocking collectives, local_step(): gram_mat = lax.psum(gram_part, 'data')  66.8 us
    dot_general x4, matrix products, local_step(): pre_act = jnp.dot(hidden, w_up[layer_idx], preferred_element_type=F32)  37 us
    dot_general x4, local copies, waits for them, and re-layouts, local_step(): pre_act = jnp.dot(hidden, w_up[layer_idx], preferred_element_type=F32)  26.9 us
    reduce_sum x20, other arithmetic, simplex_weights(): alpha_vec = alpha_vec / jnp.sum(alpha_vec)  24.6 us
    convert_element_type x2, other arithmetic, local_step(): act_bf = act_val.astype(BF16)  16.9 us
    dot_general x3, matrix products, local_step(): mlp_out = jnp.dot(act_bf, w_down[layer_idx], preferred_element_type=F32)  15.3 us
    unnamed x27, local copies, waits for them, and re-layouts  13.6 us

profile of v1, /device:TPU:1, one launch (start us, length us, event | category | flops | bytes accessed | tf_op | source)
XLA Modules:
  0.0 381.5 jit_solution(15002203824868964135)
XLA Ops:
  0.6 10.1 %fusion.10 = (f32[1024,1536]{1,0:T(8,128)}, f32[1024,1536]{1,0:T(8,128)}) fusion(bf16[1024,384]{1,0:T(8,128)(2,1)} %param.5, bf16[4,384,1536]{2,1,0:T(8,128)(2,1)} %param.7), kind=kOutput, calls=%fused_computation.22 | convolution fusion | flops 1233125376 | bytes 14548992 | tf_op jit(solution)/shard_map/dot_general | solution.py:315
  10.7 6.8 %copy.48 = f32[1024,1536]{0,1:T(8,128)} copy(f32[1024,1536]{1,0:T(8,128)} %get-tuple-element.51) | data formatting | bytes 12582912 | tf_op jit(solution)/shard_map/dot_general | solution.py:315
  17.9 5.9 %add_convert_fusion.3 = bf16[1024,384]{0,1:T(8,128)(2,1)S(1)} fusion(bf16[1024,384]{0,1:T(8,128)(2,1)S(1)} %copy.49, f32[1024,1536]{1,0:T(8,128)} %get-tuple-element.51, bf16[4,1536,384]{2,1,0:T(8,128)(2,1)} %param.8), kind=kOutput, calls=%fused_computation.97 | convolution fusion | flops 1223294976 | bytes 9043968 | tf_op jit(solution)/shard_map/dot_general | solution.py:318
  23.8 9.0 %fusion.20 = (f32[1024,1536]{1,0:T(8,128)}, f32[1024,1536]{1,0:T(8,128)}) fusion(bf16[1024,384]{0,1:T(8,128)(2,1)S(1)} %add_convert_fusion.3, bf16[4,384,1536]{2,1,0:T(8,128)(2,1)} %param.7), kind=kOutput, calls=%fused_computation.32 | convolution fusion | flops 1233125376 | bytes 14548992 | tf_op jit(solution)/shard_map/dot_general | solution.py:315
  32.8 6.8 %copy.51 = f32[1024,1536]{0,1:T(8,128)} copy(f32[1024,1536]{1,0:T(8,128)} %get-tuple-element.53) | data formatting | bytes 12582912 | tf_op jit(solution)/shard_map/dot_general | solution.py:315
  39.6 8.5 %fusion.48 = (bf16[1536,1024]{1,0:T(8,128)(2,1)}, bf16[1536,1024]{1,0:T(8,128)(2,1)}) fusion(f32[1024,1536]{0,1:T(8,128)} %copy.48, f32[1024,1536]{0,1:T(8,128)} %copy.51), kind=kLoop, calls=%fused_computation.60 | loop fusion | flops 28311552 | bytes 18874368 | tf_op jit(solution)/shard_map/convert_element_type | solution.py:317
  48.1 3.8 add_convert_fusion.2
  52.0 8.9 %fusion.30 = (f32[1024,1536]{1,0:T(8,128)}, f32[1024,1536]{1,0:T(8,128)}) fusion(bf16[1024,384]{0,1:T(8,128)(2,1)S(1)} %add_convert_fusion.2, bf16[4,384,1536]{2,1,0:T(8,128)(2,1)} %param.7), kind=kOutput, calls=%fused_computation.42 | convolution fusion | flops 1233125376 | bytes 14548992 | tf_op jit(solution)/shard_map/dot_general | solution.py:315
  60.9 6.7 %copy.53 = f32[1024,1536]{0,1:T(8,128)} copy(f32[1024,1536]{1,0:T(8,128)} %get-tuple-element.55) | data formatting | bytes 12582912 | tf_op jit(solution)/shard_map/dot_general | solution.py:315
  67.6 5.6 %add_convert_fusion.1 = bf16[1024,384]{0,1:T(8,128)(2,1)S(1)} fusion(bf16[1024,384]{0,1:T(8,128)(2,1)S(1)} %copy-done.8, f32[1024,1536]{1,0:T(8,128)} %get-tuple-element.55, bf16[4,1536,384]{2,1,0:T(8,128)(2,1)} %param.8), kind=kOutput, calls=%fused_computation.95 | convolution fusion | flops 1223294976 | bytes 9043968 | tf_op jit(solution)/shard_map/dot_general | solution.py:318
  73.2 9.0 %fusion.40 = (f32[1024,1536]{1,0:T(8,128)}, f32[1024,1536]{1,0:T(8,128)}) fusion(bf16[1024,384]{0,1:T(8,128)(2,1)S(1)} %add_convert_fusion.1, bf16[4,384,1536]{2,1,0:T(8,128)(2,1)} %param.7), kind=kOutput, calls=%fused_computation.52 | convolution fusion | flops 1233125376 | bytes 14548992 | tf_op jit(solution)/shard_map/dot_general | solution.py:315
  82.2 6.6 %copy.55 = f32[1024,1536]{0,1:T(8,128)} copy(f32[1024,1536]{1,0:T(8,128)} %get-tuple-element.57) | data formatting | bytes 12582912 | tf_op jit(solution)/shard_map/dot_general | solution.py:315
  88.8 8.4 %fusion.64 = (bf16[1536,1024]{1,0:T(8,128)(2,1)}, bf16[1536,1024]{1,0:T(8,128)(2,1)}) fusion(f32[1024,1536]{0,1:T(8,128)} %copy.53, f32[1024,1536]{0,1:T(8,128)} %copy.55), kind=kLoop, calls=%fused_computation.76 | loop fusion | flops 28311552 | bytes 18874368 | tf_op jit(solution)/shard_map/convert_element_type | solution.py:317
  97.2 6.6 %copy.57 = bf16[4,384,1536]{1,2,0:T(8,128)(2,1)} copy(bf16[4,384,1536]{2,1,0:T(8,128)(2,1)} %param.7) | data formatting | bytes 9437184 | tf_op args[2]
  103.9 6.6 %copy.58 = bf16[4,1536,384]{1,2,0:T(8,128)(2,1)} copy(bf16[4,1536,384]{2,1,0:T(8,128)(2,1)} %param.8) | data formatting | bytes 9437184 | tf_op args[3]
  110.5 5.8 %fusion.103 = f32[3,1024,13]{1,2,0:T(8,128)S(1)} fusion(bf16[3,384,13]{1,2,0:T(8,128)(2,1)S(1)} %copy-done.3, f32[1024,1536]{1,0:T(8,128)} %get-tuple-element.57, bf16[1024,384]{0,1:T(8,128)(2,1)S(1)} %add_convert_fusion.1, bf16[4,1536,384]{2,1,0:T(8,128)(2,1)} %param.8), kind=kOutput, calls=%fused_computation.123 | convolution fusion | flops 1253965824 | bytes 8447232 | tf_op jit(solution)/shard_map/bd,tdc->tbc/dot_general | solution.py:323
  116.4 2.3 convolution_convert_fusion.refs_14_
  118.7 148.7 %shard_map.84 = f32[12,72,128]{2,1,0:T(8,128)} custom-call(bf16[1536,1024]{1,0:T(8,128)(2,1)} %get-tuple-element.58.refs_0_, bf16[1536,1024]{1,0:T(8,128)(2,1)} %get-tuple-element.59.refs_1_, bf16[1536,1024]{1,0:T(8,128)(2,1)} %get-tuple-element.60.refs_2_, bf16[1536,1024]{1,0:T(8,128)(2,1)} %get-tuple-element.61.refs_3_, bf16[384,1024]{1,0:T(8,128)(2,1)} %bitcast.69, ...), custom_call_target="tpu_custom_call" | custom-call | flops 57999998976 | bytes 60000000 | tf_op jit(solution)/shard_map/pallas_call | solution.py:293
  267.4 1.2 reshape.631
  268.9 2.3 rev.3
  271.7 66.8 %psum.7 = f32[3,3]{1,0:T(4,128)S(1)} all-reduce(f32[3,3]{1,0:T(4,128)S(1)} %multiply_reduce_fusion), channel_id=1, replica_groups=mesh['data'=128] {'data'}, use_global_device_ids=true, to_apply=%region_3.0 | all-reduce | flops 9 | bytes 72 | tf_op jit(solution)/shard_map/psum | solution.py:331
  338.5 0.6 select_reduce_fusion
  340.4 0.6 broadcast_divide_fusion.19
  341.2 1.3 fusion.147
  343.2 1.3 fusion.146
  344.5 0.6 broadcast_divide_fusion.17
  345.2 1.3 fusion.145
  346.5 0.6 broadcast_divide_fusion.16
  347.3 1.3 fusion.144
  349.3 1.3 fusion.143
  350.6 0.6 broadcast_divide_fusion.14
  351.3 1.3 fusion.142
  352.6 0.6 broadcast_divide_fusion.13
  353.4 1.3 fusion.141
  355.4 1.3 fusion.140
  357.4 1.3 fusion.139
  359.5 1.3 fusion.138
  361.5 1.3 fusion.137
  363.5 1.3 fusion.136
  365.6 1.3 fusion.135
  367.6 1.3 fusion.134
  369.6 1.3 fusion.133
  371.7 1.3 fusion.132
  373.7 1.3 fusion.131
  375.7 1.3 fusion.130
  377.8 1.3 fusion.129
  379.0 1.2 broadcast_multiply_fusion.1
  380.4 0.7 fusion.149
  (65 shorter events, 13.2 us)
Async XLA Ops:
  10.7 6.8 %copy-start.1 = (bf16[1024,384]{1,0:T(8,128)(2,1)S(1)}, bf16[1024,384]{1,0:T(8,128)(2,1)}, u32[]{:S(2)}) copy-start(bf16[1024,384]{1,0:T(8,128)(2,1)} %param.5) | copy-start | bytes 2359300
  17.8 5.9 %copy-start.2 = (bf16[1024,384]{0,1:T(8,128)(2,1)}, bf16[1024,384]{0,1:T(8,128)(2,1)S(1)}, u32[]{:S(2)}) copy-start(bf16[1024,384]{0,1:T(8,128)(2,1)S(1)} %copy.49) | copy-start | bytes 2359300
  23.8 9.0 %copy-start.5 = (bf16[1024,384]{0,1:T(8,128)(2,1)}, bf16[1024,384]{0,1:T(8,128)(2,1)S(1)}, u32[]{:S(2)}) copy-start(bf16[1024,384]{0,1:T(8,128)(2,1)S(1)} %add_convert_fusion.3) | copy-start | bytes 2359300
  32.8 15.3 %slice-start = ((s8[6291456]{0:T(1024)(128)(4,1)}), s8[2097152]{0:T(1024)(128)(4,1)S(1)}, s32[]{:S(2)}) async-start(s8[6291456]{0:T(1024)(128)(4,1)} %bitcast.65), calls=%async_computation | async-start | bytes 4194304
  39.6 8.5 %slice-start.1 = ((s8[6291456]{0:T(1024)(128)(4,1)}), s8[4194304]{0:T(1024)(128)(4,1)S(1)}, s32[]{:S(2)}) async-start(s8[6291456]{0:T(1024)(128)(4,1)} %bitcast.65), calls=%async_computation.1 | async-start | bytes 8388608
  39.6 8.5 %copy-start.6 = (bf16[1024,384]{0,1:T(8,128)(2,1)S(1)}, bf16[1024,384]{0,1:T(8,128)(2,1)}, u32[]{:S(2)}) copy-start(bf16[1024,384]{0,1:T(8,128)(2,1)} %copy-done.5) | copy-start | bytes 2359300
  51.9 9.0 %copy-start.7 = (bf16[1024,384]{0,1:T(8,128)(2,1)}, bf16[1024,384]{0,1:T(8,128)(2,1)S(1)}, u32[]{:S(2)}) copy-start(bf16[1024,384]{0,1:T(8,128)(2,1)S(1)} %add_convert_fusion.2) | copy-start | bytes 2359300
  60.9 6.7 %copy-start.8 = (bf16[1024,384]{0,1:T(8,128)(2,1)S(1)}, bf16[1024,384]{0,1:T(8,128)(2,1)}, u32[]{:S(2)}) copy-start(bf16[1024,384]{0,1:T(8,128)(2,1)} %copy-done.7) | copy-start | bytes 2359300
  73.2 37.3 %copy-start.9 = (bf16[1024,384]{0,1:T(8,128)(2,1)}, bf16[1024,384]{0,1:T(8,128)(2,1)S(1)}, u32[]{:S(2)}) copy-start(bf16[1024,384]{0,1:T(8,128)(2,1)S(1)} %add_convert_fusion.1) | copy-start | bytes 2359300
  103.9 6.6 %copy-start.3 = (bf16[3,384,13]{1,2,0:T(8,128)(2,1)S(1)}, bf16[3,384,13]{1,2,0:T(8,128)(2,1)}, u32[]{:S(2)}) copy-start(bf16[3,384,13]{1,2,0:T(8,128)(2,1)} %param.9) | copy-start | bytes 89860
  110.5 5.9 %copy-start.4 = (s32[3,1024]{1,0:T(4,128)S(1)}, s32[3,1024]{1,0:T(4,128)}, u32[]{:S(2)}) copy-start(s32[3,1024]{1,0:T(4,128)} %param.6) | copy-start | bytes 36868
  338.5 42.5 %copy-start = (f32[3,3]{1,0:T(4,128)}, f32[3,3]{1,0:T(4,128)S(1)}, u32[]{:S(2)}) copy-start(f32[3,3]{1,0:T(4,128)S(1)} %psum.7) | copy-start | bytes 112

commit v2 on v1

v2 whole, which is shorter than its diff:
```python
import jax
import jax.numpy as jnp
from jax import lax
from jax.experimental import pallas as pl
from jax.experimental.pallas import tpu as pltpu
from jax.sharding import PartitionSpec as P

EG_STEPS = 20
NT = 3
NL = 4
DM = 384
DF = 1536
TOK = 1024
NC = 13
LN = 128
ROWS = 72
HALF = 36
GRP = 24
BLK = 256
GRID = (4, 4, 4)
GELU_C = 0.7978845608028654
GELU_K = 0.044715
UNITS = NT * NL
AXIS_STRIDE = (2, 8, 32)
MESH = pl.DeviceIdType.MESH
F32 = jnp.float32
BF16 = jnp.bfloat16


def half_slice(half):
    return slice(None) if half is None else pl.ds(2 * half, 2)


def step_kernel(x_hbm, lab_ref, w1_hbm, w2_hbm, heads_ref,
                alpha_ref, gram_ref, up_ref, down_ref, at_save, ht_save, sl_save,
                at, ht, sl, w1, w2, hbuf, dbuf, sbuf, ident, tmp,
                gown, gsend, rd2d, ra1, rb1, acc2, ra2, rb2, acc3, r3, res, mix, gcore, gax,
                x_sem, w_sem, save_sem, load_sem, d2d_s, d2d_r, a1_s, a1_r, b1_s, b1_r,
                a2_s, a2_r, b2_s, b2_r, c3_s, c3_r, gc_s, gc_r, gx_s, gx_r):
    me = lax.axis_index('data')
    core = lax.rem(me, 2)
    pos = [lax.rem(me // s, 4) for s in AXIS_STRIDE]
    sibling = me + 1 - 2 * core

    def at_pos(axis, k):
        return lax.rem(pos[axis] + k, 4)

    def peer(axis, k):
        return me + (at_pos(axis, k) - pos[axis]) * AXIS_STRIDE[axis]

    barrier = pltpu.get_barrier_semaphore()
    partners = [sibling] + [peer(a, k) for a in range(3) for k in (1, 2, 3)]
    for dev in partners:
        pl.semaphore_signal(barrier, inc=1, device_id=(dev,), device_id_type=MESH)

    def w_loads(layer, slot):
        return [pltpu.make_async_copy(w1_hbm.at[layer], w1.at[slot], w_sem.at[0, slot]),
                pltpu.make_async_copy(w2_hbm.at[layer], w2.at[slot], w_sem.at[1, slot])]

    def saves(layer):
        return [pltpu.make_async_copy(at.at[layer], at_save.at[layer], save_sem.at[0, layer]),
                pltpu.make_async_copy(ht.at[layer], ht_save.at[layer], save_sem.at[1, layer]),
                pltpu.make_async_copy(sl.at[layer], sl_save.at[layer], save_sem.at[2, layer])]

    def loads(layer):
        return [pltpu.make_async_copy(at_save.at[layer], at.at[layer], load_sem.at[0, layer]),
                pltpu.make_async_copy(ht_save.at[layer], ht.at[layer], load_sem.at[1, layer]),
                pltpu.make_async_copy(sl_save.at[layer], sl.at[layer], load_sem.at[2, layer])] + w_loads(layer, layer)

    x_load = pltpu.make_async_copy(x_hbm, hbuf, x_sem)
    x_load.start()
    for cp in w_loads(0, 0):
        cp.start()
    ident[...] = (lax.broadcasted_iota(jnp.int32, (256, 256), 0)
                  == lax.broadcasted_iota(jnp.int32, (256, 256), 1)).astype(F32).astype(BF16)
    x_load.wait()

    def nt_dot(a, b):
        return lax.dot_general(a, b, (((1,), (1,)), ((), ())), preferred_element_type=F32)

    def forward(layer, carry):
        slot = lax.rem(layer, 2)
        for cp in w_loads(layer, slot):
            cp.wait()

        @pl.when(layer < NL - 1)
        def _():
            for cp in w_loads(layer + 1, 1 - slot):
                cp.start()

        @pl.when(layer >= 2)
        def _():
            for cp in saves(layer - 2):
                cp.wait()

        for n in range(3):
            ht[slot, LN * n:LN * (n + 1), :] = nt_dot(
                ident[0:128, 0:128], hbuf[:, LN * n:LN * (n + 1)]).astype(BF16)

        def up(mb, c):
            rows = pl.ds(pl.multiple_of(mb * 256, 256), 256)
            for n in range(6):
                cols = slice(BLK * n, BLK * (n + 1))
                x = jnp.dot(hbuf[rows, :], w1[slot, :, cols], preferred_element_type=F32)
                x2 = x * x
                th = jnp.tanh(x * (GELU_C + (GELU_C * GELU_K) * x2))
                hp = 0.5 + 0.5 * th
                act = x * hp
                sbuf[rows, cols] = act.astype(BF16)
                sl[slot, rows, cols] = hp + act * ((1.0 - th) * (GELU_C + (3.0 * GELU_C * GELU_K) * x2))
            return c

        lax.fori_loop(0, 4, up, 0)
        for n in range(6):
            cols = slice(BLK * n, BLK * (n + 1))
            at[slot, cols, :] = nt_dot(ident[...], sbuf[:, cols]).astype(BF16)

        @pl.when(layer < 2)
        def _():
            for cp in saves(layer):
                cp.start()

        def down(mb, c):
            rows = pl.ds(pl.multiple_of(mb * 512, 512), 512)
            val = jnp.dot(sbuf[rows, :], w2[slot], preferred_element_type=F32)
            hbuf[rows, :] = (hbuf[rows, :].astype(F32) + val).astype(BF16)
            return c

        lax.fori_loop(0, 2, down, 0)
        return carry

    lax.fori_loop(0, NL, forward, 0)

    logits = nt_dot(heads_ref[...], hbuf[...])
    class_id = lax.broadcasted_iota(jnp.int32, (16, TOK), 0)
    for t in range(NT):
        lg = jnp.where(class_id < NC, logits[16 * t:16 * (t + 1), :], -jnp.inf)
        ex = jnp.exp(lg - jnp.max(lg, axis=0, keepdims=True))
        prob = ex / jnp.sum(ex, axis=0, keepdims=True)
        onehot = (class_id == lab_ref[t:t + 1, :]).astype(F32)
        err = jnp.transpose(prob - onehot).astype(BF16)
        dbuf[t] = jnp.dot(err, heads_ref[16 * t:16 * (t + 1), :], preferred_element_type=F32).astype(BF16)

    pl.semaphore_wait(barrier, len(partners))

    def remote(src, dst, send, recv, dev):
        return pltpu.make_async_remote_copy(
            src_ref=src, dst_ref=dst, send_sem=send, recv_sem=recv,
            device_id=(dev,), device_id_type=MESH)

    def chunk1(g3, p, idx, half=None):
        h, rows = half_slice(half), pl.ds(24 * p, 24)
        return (gown.at[g3, h, :, idx, rows, :], gown.at[g3, h, idx, :, rows, :],
                gown.at[g3, idx, h, :, rows, :])[p]

    def chunk2(par, p, idx, half=None):
        h = half_slice(half)
        return (acc2.at[par, 0, h, idx], acc2.at[par, 1, idx, h], acc2.at[par, 2, h, idx])[p]

    def d2d_copies(v):
        par = lax.rem(v, 2)
        return [remote(gsend.at[par], rd2d.at[par], d2d_s.at[par], d2d_r.at[par], sibling)]

    def relay1(v):
        par, g3 = lax.rem(v, 2), lax.rem(v, 3)
        return [remote(chunk1(g3, p, at_pos(p, 2), d), ra1.at[par, p, d], a1_s.at[par, p, d],
                       a1_r.at[par, p, d], peer(p, 1 + 2 * d)) for p in range(3) for d in range(2)]

    def main1(v):
        par, g3 = lax.rem(v, 2), lax.rem(v, 3)
        return [remote(chunk1(g3, p, at_pos(p, 1 + 2 * d)), rb1.at[par, p, d], b1_s.at[par, p, d],
                       b1_r.at[par, p, d], peer(p, 1 + 2 * d)) for p in range(3) for d in range(2)]

    def relay2(v):
        par = lax.rem(v, 2)
        return [remote(chunk2(par, p, at_pos((p + 1) % 3, 2), d), ra2.at[par, p, d], a2_s.at[par, p, d],
                       a2_r.at[par, p, d], peer((p + 1) % 3, 1 + 2 * d)) for p in range(3) for d in range(2)]

    def main2(v):
        par = lax.rem(v, 2)
        return [remote(chunk2(par, p, at_pos((p + 1) % 3, 1 + 2 * d)), rb2.at[par, p, d], b2_s.at[par, p, d],
                       b2_r.at[par, p, d], peer((p + 1) % 3, 1 + 2 * d)) for p in range(3) for d in range(2)]

    def last3(v):
        par = lax.rem(v, 2)
        return [remote(acc3.at[par, p, at_pos((p + 2) % 3, k)], r3.at[par, p, k - 1], c3_s.at[par, p, k - 1],
                       c3_r.at[par, p, k - 1], peer((p + 2) % 3, k)) for p in range(3) for k in (1, 2, 3)]

    def start(copies):
        for cp in copies:
            cp.start()

    def wait(copies):
        for cp in copies:
            cp.wait()

    def step_d2d(v):
        wait(d2d_copies(v))
        par, g3 = lax.rem(v, 2), lax.rem(v, 3)

        def add(i, carry):
            gown[g3, i] = gown[g3, i] + rd2d[par, i]
            return carry

        lax.fori_loop(0, 4, add, 0)
        start(relay1(v))

    def step_relay1(v):
        wait(relay1(v))
        par, g3 = lax.rem(v, 2), lax.rem(v, 3)
        for p in range(3):
            for d in range(2):
                dst = chunk1(g3, p, at_pos(p, 1 + 2 * d), d)
                dst[...] = dst[...] + ra1[par, p, d]
        start(main1(v))

    def step_main1(v):
        wait(main1(v))
        par, g3 = lax.rem(v, 2), lax.rem(v, 3)
        for p in range(3):
            acc2[par, p] = chunk1(g3, p, pos[p])[...] + rb1[par, p, 0] + rb1[par, p, 1]
        start(relay2(v))

    def step_relay2(v):
        wait(relay2(v))
        par = lax.rem(v, 2)
        for p in range(3):
            for d in range(2):
                dst = chunk2(par, p, at_pos((p + 1) % 3, 1 + 2 * d), d)
                dst[...] = dst[...] + ra2[par, p, d]
        start(main2(v))

    def step_main2(v):
        wait(main2(v))
        par = lax.rem(v, 2)
        for p in range(3):
            acc3[par, p] = chunk2(par, p, pos[(p + 1) % 3])[...] + rb2[par, p, 0] + rb2[par, p, 1]
        start(last3(v))

    def step_last3(v):
        wait(last3(v))
        par = lax.rem(v, 2)
        for p in range(3):
            res[v, pl.ds(24 * p, 24), :] = (
                (acc3[par, p, pos[(p + 2) % 3]] + r3[par, p, 0]) + (r3[par, p, 1] + r3[par, p, 2]))

    def when_unit(v, step):
        pl.when(jnp.logical_and(v >= 0, v < UNITS))(lambda: step(v))

    def body(u, carry):
        li, task = u // NT, lax.rem(u, NT)
        slot = lax.rem(li + 1, 2)
        par, g3 = lax.rem(u, 2), lax.rem(u, 3)
        computing = u < UNITS

        def dest(rel):
            if rel == 0:
                return gown.at[g3].reshape(64 * ROWS, LN)
            return gsend.at[par].reshape(64 * ROWS, LN)

        for k in (2, 3):
            @pl.when(u == NT * (k - 1))
            def _(k=k):
                for cp in loads(NL - 1 - k):
                    cp.start()

            @pl.when(u == NT * k)
            def _(k=k):
                for cp in loads(NL - 1 - k):
                    cp.wait()

        @pl.when(computing)
        def _():
            for m in range(4):
                val = jnp.dot(at[slot, 384 * m:384 * (m + 1), :], dbuf[task], preferred_element_type=F32)
                for lb in range(3):
                    tmp[m % 2, lb] = val[:, LN * lb:LN * (lb + 1)]
                for rel in range(2):
                    cc = core if rel == 0 else 1 - core
                    dst = dest(rel)
                    for j in range(12):
                        for lb in range(3):
                            dst[pl.ds(m * 16 * 72 + 36 + 3 * j + lb, 16, stride=ROWS), :] = (
                                tmp[m % 2, lb, pl.ds(12 * cc + j, 16, stride=24), :])

        when_unit(u - 3, step_relay2)
        when_unit(u - 4, step_last3)

        @pl.when(computing)
        def _():
            def block(mb, c):
                rows = pl.ds(pl.multiple_of(mb * 512, 512), 512)
                for n in range(6):
                    cols = slice(BLK * n, BLK * (n + 1))
                    val = nt_dot(dbuf[task, rows, :], w2[slot, cols, :])
                    sbuf[rows, cols] = (val * sl[slot, rows, cols]).astype(BF16)
                return c
            lax.fori_loop(0, 2, block, 0)

        when_unit(u - 1, step_d2d)

        @pl.when(computing)
        def _():
            for n in range(6):
                val = jnp.dot(ht[slot], sbuf[:, BLK * n:BLK * (n + 1)], preferred_element_type=F32)
                for lb in range(2):
                    tmp[n % 2, lb] = val[:, LN * lb:LN * (lb + 1)]
                for rel in range(2):
                    cc = core if rel == 0 else 1 - core
                    dst = dest(rel)
                    for r in range(3):
                        for lb in range(2):
                            dst[pl.ds(12 * r + 2 * n + lb, 64, stride=ROWS), :] = (
                                tmp[n % 2, lb, pl.ds(3 * cc + r, 64, stride=6), :])

        when_unit(u, lambda v: start(d2d_copies(v)))
        when_unit(u - 3, step_main2)
        when_unit(u - 2, step_main1)

        @pl.when(u < UNITS - NT)
        def _():
            def block(mb, c):
                rows = pl.ds(pl.multiple_of(mb * 512, 512), 512)
                val = nt_dot(sbuf[rows, :], w1[slot])
                dbuf[task, rows, :] = (dbuf[task, rows, :].astype(F32) + val).astype(BF16)
                return c
            lax.fori_loop(0, 2, block, 0)

        when_unit(u - 1, step_relay1)
        return carry

    lax.fori_loop(0, UNITS + 4, body, 0)

    inv_tokens = 1.0 / (TOK * lax.axis_size('data'))
    pairs = [(t, s) for t in range(NT) for s in range(t, NT)]
    rows6 = []
    for t, s in pairs:
        prod = res[t] * res[s]
        for li in range(1, NL):
            prod = prod + res[NT * li + t] * res[NT * li + s]
        rows6.append(jnp.sum(prod, axis=0, keepdims=True))
    tile = jnp.concatenate(rows6 + [jnp.zeros((2, 128), F32)], axis=0) * (inv_tokens * inv_tokens)

    gcore[core] = tile
    cp = remote(gcore.at[core], gcore.at[core], gc_s, gc_r, sibling)
    cp.start()
    cp.wait()
    tile = gcore[0] + gcore[1]
    for a in range(3):
        gax[a, pos[a]] = tile
        copies = [remote(gax.at[a, pos[a]], gax.at[a, pos[a]], gx_s.at[a, k - 1], gx_r.at[a, k - 1], peer(a, k))
                  for k in (1, 2, 3)]
        start(copies)
        wait(copies)
        tile = (gax[a, 0] + gax[a, 1]) + (gax[a, 2] + gax[a, 3])

    sums = jnp.broadcast_to(jnp.sum(tile, axis=1, keepdims=True), (8, LN))
    gram = {}
    for i, (t, s) in enumerate(pairs):
        gram[t, s] = gram[s, t] = jnp.broadcast_to(sums[i:i + 1, :], (8, LN))
    temperature = (gram[0, 0] + gram[1, 1] + gram[2, 2]) / NT
    alpha = [jnp.full((8, LN), 1.0 / NT, F32)] * NT

    def eg_step(i, alpha):
        pull = [gram[t, 0] * alpha[0] + gram[t, 1] * alpha[1] + gram[t, 2] * alpha[2] for t in range(NT)]
        new = [alpha[t] * jnp.exp(-pull[t] / temperature) for t in range(NT)]
        total = new[0] + new[1] + new[2]
        return tuple(a / total for a in new)

    alpha = lax.fori_loop(0, EG_STEPS, eg_step, tuple(alpha))
    for t in range(NT):
        alpha_ref[t] = alpha[t][0, 0]
        for s in range(NT):
            gram_ref[t, s] = gram[t, s][0, 0]
    scale = [jnp.broadcast_to(alpha[t][0:1, :] * inv_tokens, (72, 128)) for t in range(NT)]
    for layer in range(NL):
        u = NT * (NL - 1 - layer)
        mix[72 * layer:72 * (layer + 1), :] = scale[0] * res[u] + scale[1] * res[u + 1] + scale[2] * res[u + 2]
    for k in range(36):
        up_ref[:, LN * k:LN * (k + 1)] = mix[pl.ds(k, NL, stride=ROWS), :]
        down_ref[:, LN * k:LN * (k + 1)] = mix[pl.ds(36 + k, NL, stride=ROWS), :]


def whole_step(x, labels, w_up, w_down, heads_t):
    any_spec = pl.BlockSpec(memory_space=pl.ANY)
    vmem_spec = pl.BlockSpec(memory_space=pltpu.VMEM)
    smem_spec = pl.BlockSpec(memory_space=pltpu.SMEM)
    dma = pltpu.SemaphoreType.DMA
    two, three = (2,), (3,)

    def vmem(*shape, dtype=F32):
        return pltpu.VMEM(shape, dtype)

    both = pltpu.SemaphoreType.DMA(two + three + two)
    triple = dma(three + three)
    scratch = [
        vmem(2, DF, TOK, dtype=BF16),
        vmem(2, DM, TOK, dtype=BF16),
        vmem(2, TOK, DF),
        vmem(2, DM, DF, dtype=BF16),
        vmem(2, DF, DM, dtype=BF16),
        vmem(TOK, DM, dtype=BF16),
        vmem(NT, TOK, DM, dtype=BF16),
        vmem(TOK, DF, dtype=BF16),
        vmem(BLK, BLK, dtype=BF16),
        vmem(2, 3, DM, LN),
        vmem(3, *GRID, ROWS, LN),
        vmem(2, *GRID, ROWS, LN),
        vmem(2, *GRID, ROWS, LN),
        vmem(2, 3, 2, 2, 4, GRP, LN),
        vmem(2, 3, 2, 4, 4, GRP, LN),
        vmem(2, 3, 4, 4, GRP, LN),
        vmem(2, 3, 2, 2, GRP, LN),
        vmem(2, 3, 2, 4, GRP, LN),
        vmem(2, 3, 4, GRP, LN),
        vmem(2, 3, 3, GRP, LN),
        vmem(UNITS, ROWS, LN),
        vmem(NL * ROWS, LN),
        vmem(2, 8, LN),
        vmem(3, 4, 8, LN),
        dma, dma(two + two), dma(three + two), dma(three + two), dma(two), dma(two),
        both, both, both, both, both, both, both, both,
        dma(two + three + three), dma(two + three + three), dma, dma, triple, triple,
    ]
    return pl.pallas_call(
        step_kernel,
        out_shape=(
            jax.ShapeDtypeStruct((NT,), F32),
            jax.ShapeDtypeStruct((NT, NT), F32),
            jax.ShapeDtypeStruct((NL, HALF * LN), F32),
            jax.ShapeDtypeStruct((NL, HALF * LN), F32),
            jax.ShapeDtypeStruct((2, DF, TOK), BF16),
            jax.ShapeDtypeStruct((2, DM, TOK), BF16),
            jax.ShapeDtypeStruct((2, TOK, DF), F32),
        ),
        in_specs=[any_spec, vmem_spec, any_spec, any_spec, vmem_spec],
        out_specs=(smem_spec, smem_spec, vmem_spec, vmem_spec, any_spec, any_spec, any_spec),
        scratch_shapes=scratch,
        compiler_params=pltpu.CompilerParams(
            collective_id=0, has_side_effects=True, vmem_limit_bytes=67043328),
    )(x, labels, w_up, w_down, heads_t)[:4]


def solution(mesh):
    def local_step(x_local, lab_local, w_up, w_down, task_heads):
        heads_t = jnp.pad(jnp.swapaxes(task_heads, 1, 2), ((0, 0), (0, 16 - NC), (0, 0))).reshape(NT * 16, DM)
        return whole_step(x_local, lab_local, w_up, w_down, heads_t)

    return jax.shard_map(local_step, mesh=mesh, in_specs=(P('data', None), P(None, 'data'), P(), P(), P()), out_specs=(P(), P(), P(None, 'data'), P(None, 'data')), check_vma=False)
```

time: 386 us -> 200 us (0.52)
  blocking collectives: 66.8 us -> 0 us
  matrix products: 60.4 us -> 0 us
  other arithmetic: 58.5 us -> 0 us
  Pallas kernels: 149 us -> 192 us
  local copies, waits for them, and re-layouts: 45 us -> 6.8 us
    psum x1 -> x0, blocking collectives: 66.8 us -> none  [local_step(): gram_mat = lax.psum(gram_part, 'data')]
    dot_general x9 -> x0, matrix products: 60.4 us -> none  [the longest x4 37 us: local_step(): pre_act = jnp.dot(hidden, w_up[layer_idx], preferred_element_type=F32)]
    pallas_call x1, Pallas kernels: 149 us -> 192 us  [whole_step(): pl.pallas_call(step_kernel, out_shape=(jax.ShapeDtypeStruct((NT,), F32),...]
    reduce_sum x42 -> x0, other arithmetic: 27.9 us -> none  [the longest x20 24.6 us: simplex_weights(): alpha_vec = alpha_vec / jnp.sum(alpha_vec)]
    dot_general x4 -> x0, local copies, waits for them, and re-layouts: 26.9 us -> none  [local_step(): pre_act = jnp.dot(hidden, w_up[layer_idx], preferred_element_type=F32)]
    convert_element_type x2 -> x0, other arithmetic: 16.9 us -> none  [local_step(): act_bf = act_val.astype(BF16)]
    div x19 -> x0, other arithmetic: 12.3 us -> none  [simplex_weights(): alpha_vec = alpha_vec / jnp.sum(alpha_vec)]
    unnamed x27 -> x4, local copies, waits for them, and re-layouts: 13.6 us -> 5.41 us
where the time goes in v2:
time: 200 us; the launch traced here: 199 us
  Pallas kernels  192 us (96%)
  local copies, waits for them, and re-layouts  6.8 us (3%)
    pallas_call x1, Pallas kernels, whole_step(): pl.pallas_call(step_kernel, out_shape=(jax.ShapeDtypeStruct((NT,), F32),...  192 us
    unnamed x4, local copies, waits for them, and re-layouts  5.41 us

profile of v2, /device:TPU:1, one launch (start us, length us, event | category | flops | bytes accessed | tf_op | source)
XLA Modules:
  0.0 199.0 jit_solution(11739830732838231492)
XLA Ops:
  0.6 1.4 pad.4
  2.0 191.5 %shard_map.84 = (f32[3]{0:T(128)}, f32[3,3]{1,0:T(4,128)}, f32[4,4608]{1,0:T(4,128)}, f32[4,4608]{1,0:T(4,128)}, bf16[2,1536,1024]{2,1,0:T(8,128)(2,1)}, /*index...) custom-call(bf16[1024,384]{1,0:T(8,128)(2,1)} %x_hbm.1, s32[3,1024]{1,0:T(4,128)} %lab_ref.1, ...), custom_call_target="tpu_custom_call" | custom-call | tf_op jit(solution)/shard_map/pallas_call | solution.py:425
  193.6 1.1 copy.13
  194.7 1.3 copy.14
  195.9 1.5 copy.15
  197.5 1.5 copy.16

commit v3 on v2

--- a/solution.py
+++ b/solution.py
@@ -21,6 +21,7 @@
 GELU_C = 0.7978845608028654
 GELU_K = 0.044715
 UNITS = NT * NL
+DUE = (5, 8, 11, 14, 17, 20)
 AXIS_STRIDE = (2, 8, 32)
 MESH = pl.DeviceIdType.MESH
 F32 = jnp.float32
@@ -36,7 +37,7 @@
                 at, ht, sl, w1, w2, hbuf, dbuf, sbuf, ident, tmp,
                 gown, gsend, rd2d, ra1, rb1, acc2, ra2, rb2, acc3, r3, res, mix, gcore, gax,
                 x_sem, w_sem, save_sem, load_sem, d2d_s, d2d_r, a1_s, a1_r, b1_s, b1_r,
-                a2_s, a2_r, b2_s, b2_r, c3_s, c3_r, gc_s, gc_r, gx_s, gx_r):
+                a2_s, a2_r, b2_s, b2_r, c3_s, c3_r, e1_s, e1_r, e2_s, e2_r, gc_s, gc_r, gx_s, gx_r):
     me = lax.axis_index('data')
     core = lax.rem(me, 2)
     pos = [lax.rem(me // s, 4) for s in AXIS_STRIDE]
@@ -49,7 +50,9 @@
         return me + (at_pos(axis, k) - pos[axis]) * AXIS_STRIDE[axis]
 
     barrier = pltpu.get_barrier_semaphore()
-    partners = [sibling] + [peer(a, k) for a in range(3) for k in (1, 2, 3)]
+    row_peers = [sibling] + [dev + c * (sibling - me) for dev in (peer(0, 1), peer(0, 2), peer(0, 3)) for c in range(2)]
+    plane_peers = [me + peer(1, j) - me + peer(2, k) - me for k in range(4) for j in range(4) if j + k]
+    partners = row_peers + plane_peers
     for dev in partners:
         pl.semaphore_signal(barrier, inc=1, device_id=(dev,), device_id_type=MESH)
 
@@ -98,7 +101,7 @@
                 ident[0:128, 0:128], hbuf[:, LN * n:LN * (n + 1)]).astype(BF16)
 
         def up(mb, c):
-            rows = pl.ds(pl.multiple_of(mb * 256, 256), 256)
+            rows = slice(None)
             for n in range(6):
                 cols = slice(BLK * n, BLK * (n + 1))
                 x = jnp.dot(hbuf[rows, :], w1[slot, :, cols], preferred_element_type=F32)
@@ -110,7 +113,7 @@
                 sl[slot, rows, cols] = hp + act * ((1.0 - th) * (GELU_C + (3.0 * GELU_C * GELU_K) * x2))
             return c
 
-        lax.fori_loop(0, 4, up, 0)
+        up(0, 0)
         for n in range(6):
             cols = slice(BLK * n, BLK * (n + 1))
             at[slot, cols, :] = nt_dot(ident[...], sbuf[:, cols]).astype(BF16)
@@ -121,12 +124,12 @@
                 cp.start()
 
         def down(mb, c):
-            rows = pl.ds(pl.multiple_of(mb * 512, 512), 512)
+            rows = slice(None)
             val = jnp.dot(sbuf[rows, :], w2[slot], preferred_element_type=F32)
             hbuf[rows, :] = (hbuf[rows, :].astype(F32) + val).astype(BF16)
             return c
 
-        lax.fori_loop(0, 2, down, 0)
+        down(0, 0)
         return carry
 
     lax.fori_loop(0, NL, forward, 0)
@@ -162,29 +165,53 @@
         return [remote(gsend.at[par], rd2d.at[par], d2d_s.at[par], d2d_r.at[par], sibling)]
 
     def relay1(v):
-        par, g3 = lax.rem(v, 2), lax.rem(v, 3)
+        par = g3 = lax.rem(v, 3)
         return [remote(chunk1(g3, p, at_pos(p, 2), d), ra1.at[par, p, d], a1_s.at[par, p, d],
                        a1_r.at[par, p, d], peer(p, 1 + 2 * d)) for p in range(3) for d in range(2)]
 
+    def direct1(v):
+        par = g3 = lax.rem(v, 3)
+        return [remote(chunk1(g3, p, at_pos(p, 1 + 2 * d), 1 - d), rb1.at[par, p, d, half_slice(1 - d)],
+                       e1_s.at[par, p, d], e1_r.at[par, p, d], peer(p, 1 + 2 * d)) for p in range(3) for d in range(2)]
+
     def main1(v):
-        par, g3 = lax.rem(v, 2), lax.rem(v, 3)
-        return [remote(chunk1(g3, p, at_pos(p, 1 + 2 * d)), rb1.at[par, p, d], b1_s.at[par, p, d],
+        par = g3 = lax.rem(v, 3)
+        return [remote(chunk1(g3, p, at_pos(p, 1 + 2 * d), d), rb1.at[par, p, d, half_slice(d)], b1_s.at[par, p, d],
                        b1_r.at[par, p, d], peer(p, 1 + 2 * d)) for p in range(3) for d in range(2)]
 
     def relay2(v):
-        par = lax.rem(v, 2)
+        par = lax.rem(v, 3)
         return [remote(chunk2(par, p, at_pos((p + 1) % 3, 2), d), ra2.at[par, p, d], a2_s.at[par, p, d],
                        a2_r.at[par, p, d], peer((p + 1) % 3, 1 + 2 * d)) for p in range(3) for d in range(2)]
 
+    def direct2(v):
+        par = lax.rem(v, 3)
+        return [remote(chunk2(par, p, at_pos((p + 1) % 3, 1 + 2 * d), 1 - d), rb2.at[par, p, d, half_slice(1 - d)],
+                       e2_s.at[par, p, d], e2_r.at[par, p, d], peer((p + 1) % 3, 1 + 2 * d))
+                for p in range(3) for d in range(2)]
+
     def main2(v):
-        par = lax.rem(v, 2)
-        return [remote(chunk2(par, p, at_pos((p + 1) % 3, 1 + 2 * d)), rb2.at[par, p, d], b2_s.at[par, p, d],
-                       b2_r.at[par, p, d], peer((p + 1) % 3, 1 + 2 * d)) for p in range(3) for d in range(2)]
+        par = lax.rem(v, 3)
+        return [remote(chunk2(par, p, at_pos((p + 1) % 3, 1 + 2 * d), d), rb2.at[par, p, d, half_slice(d)],
+                       b2_s.at[par, p, d], b2_r.at[par, p, d], peer((p + 1) % 3, 1 + 2 * d))
+                for p in range(3) for d in range(2)]
 
     def last3(v):
-        par = lax.rem(v, 2)
+        par = lax.rem(v, 3)
         return [remote(acc3.at[par, p, at_pos((p + 2) % 3, k)], r3.at[par, p, k - 1], c3_s.at[par, p, k - 1],
                        c3_r.at[par, p, k - 1], peer((p + 2) % 3, k)) for p in range(3) for k in (1, 2, 3)]
+
+    def share(peers, slot, send, recv):
+        copies = [remote(slot, slot, send.at[i], recv.at[i], dev) for i, dev in enumerate(peers)]
+        for cp in copies:
+            cp.start()
+        for cp in copies:
+            cp.wait()
+
+    def tree_sum(terms):
+        while len(terms) > 1:
+            terms = [a + b for a, b in zip(terms[::2], terms[1::2])]
+        return terms[0]
 
     def start(copies):
         for cp in copies:
@@ -203,11 +230,11 @@
             return carry
 
         lax.fori_loop(0, 4, add, 0)
-        start(relay1(v))
+        start(relay1(v) + direct1(v))
 
     def step_relay1(v):
         wait(relay1(v))
-        par, g3 = lax.rem(v, 2), lax.rem(v, 3)
+        par = g3 = lax.rem(v, 3)
         for p in range(3):
             for d in range(2):
                 dst = chunk1(g3, p, at_pos(p, 1 + 2 * d), d)
@@ -215,15 +242,15 @@
         start(main1(v))
 
     def step_main1(v):
-        wait(main1(v))
-        par, g3 = lax.rem(v, 2), lax.rem(v, 3)
+        wait(main1(v) + direct1(v))
+        par = g3 = lax.rem(v, 3)
         for p in range(3):
             acc2[par, p] = chunk1(g3, p, pos[p])[...] + rb1[par, p, 0] + rb1[par, p, 1]
-        start(relay2(v))
+        start(relay2(v) + direct2(v))
 
     def step_relay2(v):
         wait(relay2(v))
-        par = lax.rem(v, 2)
+        par = lax.rem(v, 3)
         for p in range(3):
             for d in range(2):
                 dst = chunk2(par, p, at_pos((p + 1) % 3, 1 + 2 * d), d)
@@ -231,21 +258,28 @@
         start(main2(v))
 
     def step_main2(v):
-        wait(main2(v))
-        par = lax.rem(v, 2)
+        wait(main2(v) + direct2(v))
+        par = lax.rem(v, 3)
         for p in range(3):
             acc3[par, p] = chunk2(par, p, pos[(p + 1) % 3])[...] + rb2[par, p, 0] + rb2[par, p, 1]
         start(last3(v))
 
     def step_last3(v):
         wait(last3(v))
-        par = lax.rem(v, 2)
+        par = lax.rem(v, 3)
         for p in range(3):
             res[v, pl.ds(24 * p, 24), :] = (
                 (acc3[par, p, pos[(p + 2) % 3]] + r3[par, p, 0]) + (r3[par, p, 1] + r3[par, p, 2]))
 
     def when_unit(v, step):
         pl.when(jnp.logical_and(v >= 0, v < UNITS))(lambda: step(v))
+
+    steps = (step_d2d, step_relay1, step_main1, step_relay2, step_main2, step_last3)
+
+    def run_slot(u, k):
+        for due, step in reversed(tuple(zip(DUE, steps))):
+            if due % 4 == k:
+                when_unit(u - due // 4, step)
 
     def body(u, carry):
         li, task = u // NT, lax.rem(u, NT)
@@ -283,21 +317,20 @@
                             dst[pl.ds(m * 16 * 72 + 36 + 3 * j + lb, 16, stride=ROWS), :] = (
                                 tmp[m % 2, lb, pl.ds(12 * cc + j, 16, stride=24), :])
 
-        when_unit(u - 3, step_relay2)
-        when_unit(u - 4, step_last3)
+        run_slot(u, 0)
 
         @pl.when(computing)
         def _():
             def block(mb, c):
-                rows = pl.ds(pl.multiple_of(mb * 512, 512), 512)
+                rows = slice(None)
                 for n in range(6):
                     cols = slice(BLK * n, BLK * (n + 1))
                     val = nt_dot(dbuf[task, rows, :], w2[slot, cols, :])
                     sbuf[rows, cols] = (val * sl[slot, rows, cols]).astype(BF16)
                 return c
-            lax.fori_loop(0, 2, block, 0)
-
-        when_unit(u - 1, step_d2d)
+            block(0, 0)
+
+        run_slot(u, 1)
 
         @pl.when(computing)
         def _():
@@ -314,22 +347,21 @@
                                 tmp[n % 2, lb, pl.ds(3 * cc + r, 64, stride=6), :])
 
         when_unit(u, lambda v: start(d2d_copies(v)))
-        when_unit(u - 3, step_main2)
-        when_unit(u - 2, step_main1)
+        run_slot(u, 2)
 
         @pl.when(u < UNITS - NT)
         def _():
             def block(mb, c):
-                rows = pl.ds(pl.multiple_of(mb * 512, 512), 512)
+                rows = slice(None)
                 val = nt_dot(sbuf[rows, :], w1[slot])
                 dbuf[task, rows, :] = (dbuf[task, rows, :].astype(F32) + val).astype(BF16)
                 return c
-            lax.fori_loop(0, 2, block, 0)
-
-        when_unit(u - 1, step_relay1)
+            block(0, 0)
+
+        run_slot(u, 3)
         return carry
 
-    lax.fori_loop(0, UNITS + 4, body, 0)
+    lax.fori_loop(0, UNITS + DUE[-1] // 4, body, 0)
 
     inv_tokens = 1.0 / (TOK * lax.axis_size('data'))
     pairs = [(t, s) for t in range(NT) for s in range(t, NT)]
@@ -341,18 +373,13 @@
         rows6.append(jnp.sum(prod, axis=0, keepdims=True))
     tile = jnp.concatenate(rows6 + [jnp.zeros((2, 128), F32)], axis=0) * (inv_tokens * inv_tokens)
 
-    gcore[core] = tile
-    cp = remote(gcore.at[core], gcore.at[core], gc_s, gc_r, sibling)
-    cp.start()
-    cp.wait()
-    tile = gcore[0] + gcore[1]
-    for a in range(3):
-        gax[a, pos[a]] = tile
-        copies = [remote(gax.at[a, pos[a]], gax.at[a, pos[a]], gx_s.at[a, k - 1], gx_r.at[a, k - 1], peer(a, k))
-                  for k in (1, 2, 3)]
-        start(copies)
-        wait(copies)
-        tile = (gax[a, 0] + gax[a, 1]) + (gax[a, 2] + gax[a, 3])
+    row_id, plane_id = 2 * pos[0] + core, 4 * pos[2] + pos[1]
+    gcore[row_id] = tile
+    share(row_peers, gcore.at[row_id], gc_s, gc_r)
+    tile = tree_sum([gcore[i] for i in range(8)])
+    gax[plane_id] = tile
+    share(plane_peers, gax.at[plane_id], gx_s, gx_r)
+    tile = tree_sum([gax[i] for i in range(16)])
 
     sums = jnp.broadcast_to(jnp.sum(tile, axis=1, keepdims=True), (8, LN))
     gram = {}
@@ -391,8 +418,8 @@
     def vmem(*shape, dtype=F32):
         return pltpu.VMEM(shape, dtype)
 
-    both = pltpu.SemaphoreType.DMA(two + three + two)
-    triple = dma(three + three)
+    both = pltpu.SemaphoreType.DMA(three + three + two)
+    triple = dma(three + three + three)
     scratch = [
         vmem(2, DF, TOK, dtype=BF16),
         vmem(2, DM, TOK, dtype=BF16),
@@ -407,20 +434,20 @@
         vmem(3, *GRID, ROWS, LN),
         vmem(2, *GRID, ROWS, LN),
         vmem(2, *GRID, ROWS, LN),
-        vmem(2, 3, 2, 2, 4, GRP, LN),
-        vmem(2, 3, 2, 4, 4, GRP, LN),
-        vmem(2, 3, 4, 4, GRP, LN),
-        vmem(2, 3, 2, 2, GRP, LN),
-        vmem(2, 3, 2, 4, GRP, LN),
-        vmem(2, 3, 4, GRP, LN),
-        vmem(2, 3, 3, GRP, LN),
+        vmem(3, 3, 2, 2, 4, GRP, LN),
+        vmem(3, 3, 2, 4, 4, GRP, LN),
+        vmem(3, 3, 4, 4, GRP, LN),
+        vmem(3, 3, 2, 2, GRP, LN),
+        vmem(3, 3, 2, 4, GRP, LN),
+        vmem(3, 3, 4, GRP, LN),
+        vmem(3, 3, 3, GRP, LN),
         vmem(UNITS, ROWS, LN),
         vmem(NL * ROWS, LN),
-        vmem(2, 8, LN),
-        vmem(3, 4, 8, LN),
+        vmem(8, 8, LN),
+        vmem(16, 8, LN),
         dma, dma(two + two), dma(three + two), dma(three + two), dma(two), dma(two),
         both, both, both, both, both, both, both, both,
-        dma(two + three + three), dma(two + three + three), dma, dma, triple, triple,
+        triple, triple, both, both, both, both, dma((7,)), dma((7,)), dma((15,)), dma((15,)),
     ]
     return pl.pallas_call(
         step_kernel,

time: 200 us -> 186 us (0.930)
  Pallas kernels: 192 us -> 178 us
    pallas_call x1, Pallas kernels: 192 us -> 178 us  [whole_step(): pl.pallas_call(step_kernel, out_shape=(jax.ShapeDtypeStruct((NT,), F32),...]
where the time goes in v3:
time: 186 us; the launch traced here: 185 us
  Pallas kernels  178 us (96%)
  local copies, waits for them, and re-layouts  6.8 us (4%)
    pallas_call x1, Pallas kernels, whole_step(): pl.pallas_call(step_kernel, out_shape=(jax.ShapeDtypeStruct((NT,), F32),...  178 us
    unnamed x4, local copies, waits for them, and re-layouts  5.41 us

profile of v3, /device:TPU:1, one launch (start us, length us, event | category | flops | bytes accessed | tf_op | source)
XLA Modules:
  0.0 185.4 jit_solution(5407017021965969290)
XLA Ops:
  0.6 1.4 pad.4
  2.0 177.9 %shard_map.84 = (f32[3]{0:T(128)}, f32[3,3]{1,0:T(4,128)}, f32[4,4608]{1,0:T(4,128)}, f32[4,4608]{1,0:T(4,128)}, bf16[2,1536,1024]{2,1,0:T(8,128)(2,1)}, /*index...) custom-call(bf16[1024,384]{1,0:T(8,128)(2,1)} %x_hbm.1, s32[3,1024]{1,0:T(4,128)} %lab_ref.1, ...), custom_call_target="tpu_custom_call" | custom-call | tf_op jit(solution)/shard_map/pallas_call | solution.py:452
  180.0 1.1 copy.13
  181.1 1.3 copy.14
  182.3 1.5 copy.15
  183.8 1.5 copy.16

commit v4 on v3

--- a/solution.py
+++ b/solution.py
@@ -34,7 +34,7 @@
 
 def step_kernel(x_hbm, lab_ref, w1_hbm, w2_hbm, heads_ref,
                 alpha_ref, gram_ref, up_ref, down_ref, at_save, ht_save, sl_save,
-                at, ht, sl, w1, w2, hbuf, dbuf, sbuf, ident, tmp,
+                at, ht, sl, w1, w2, hbuf, dbuf, sbuf, tmp,
                 gown, gsend, rd2d, ra1, rb1, acc2, ra2, rb2, acc3, r3, res, mix, gcore, gax,
                 x_sem, w_sem, save_sem, load_sem, d2d_s, d2d_r, a1_s, a1_r, b1_s, b1_r,
                 a2_s, a2_r, b2_s, b2_r, c3_s, c3_r, e1_s, e1_r, e2_s, e2_r, gc_s, gc_r, gx_s, gx_r):
@@ -74,8 +74,6 @@
     x_load.start()
     for cp in w_loads(0, 0):
         cp.start()
-    ident[...] = (lax.broadcasted_iota(jnp.int32, (256, 256), 0)
-                  == lax.broadcasted_iota(jnp.int32, (256, 256), 1)).astype(F32).astype(BF16)
     x_load.wait()
 
     def nt_dot(a, b):
@@ -97,8 +95,7 @@
                 cp.wait()
 
         for n in range(3):
-            ht[slot, LN * n:LN * (n + 1), :] = nt_dot(
-                ident[0:128, 0:128], hbuf[:, LN * n:LN * (n + 1)]).astype(BF16)
+            ht[slot, LN * n:LN * (n + 1), :] = hbuf[:, LN * n:LN * (n + 1)].T
 
         def up(mb, c):
             rows = slice(None)
@@ -116,7 +113,7 @@
         up(0, 0)
         for n in range(6):
             cols = slice(BLK * n, BLK * (n + 1))
-            at[slot, cols, :] = nt_dot(ident[...], sbuf[:, cols]).astype(BF16)
+            at[slot, cols, :] = sbuf[:, cols].T
 
         @pl.when(layer < 2)
         def _():
@@ -162,7 +159,8 @@
 
     def d2d_copies(v):
         par = lax.rem(v, 2)
-        return [remote(gsend.at[par], rd2d.at[par], d2d_s.at[par], d2d_r.at[par], sibling)]
+        part = [(par, slice(None), slice(None), slice(None), pl.ds(GRP * p, GRP)) for p in range(3)]
+        return [remote(gsend.at[part[p]], rd2d.at[part[p]], d2d_s.at[par, p], d2d_r.at[par, p], sibling) for p in range(3)]
 
     def relay1(v):
         par = g3 = lax.rem(v, 3)
@@ -222,47 +220,58 @@
             cp.wait()
 
     def step_d2d(v):
-        wait(d2d_copies(v))
         par, g3 = lax.rem(v, 2), lax.rem(v, 3)
-
-        def add(i, carry):
-            gown[g3, i] = gown[g3, i] + rd2d[par, i]
-            return carry
-
-        lax.fori_loop(0, 4, add, 0)
-        start(relay1(v) + direct1(v))
+        relays, directs = relay1(v), direct1(v)
+        for p, cp in enumerate(d2d_copies(v)):
+            cp.wait()
+
+            def add(i, carry, p=p):
+                rows = pl.ds(GRP * p, GRP)
+                gown[g3, i, :, :, rows, :] = gown[g3, i, :, :, rows, :] + rd2d[par, i, :, :, rows, :]
+                return carry
+
+            lax.fori_loop(0, 4, add, 0)
+            start(relays[2 * p:2 * p + 2])
+        start(directs)
 
     def step_relay1(v):
-        wait(relay1(v))
         par = g3 = lax.rem(v, 3)
+        relays, mains = relay1(v), main1(v)
         for p in range(3):
             for d in range(2):
+                relays[2 * p + d].wait()
                 dst = chunk1(g3, p, at_pos(p, 1 + 2 * d), d)
                 dst[...] = dst[...] + ra1[par, p, d]
-        start(main1(v))
+                mains[2 * p + d].start()
 
     def step_main1(v):
-        wait(main1(v) + direct1(v))
         par = g3 = lax.rem(v, 3)
+        mains, early, relays, directs = main1(v), direct1(v), relay2(v), direct2(v)
         for p in range(3):
+            pair = slice(2 * p, 2 * p + 2)
+            wait(early[pair] + mains[pair])
             acc2[par, p] = chunk1(g3, p, pos[p])[...] + rb1[par, p, 0] + rb1[par, p, 1]
-        start(relay2(v) + direct2(v))
+            start(relays[pair])
+        start(directs)
 
     def step_relay2(v):
-        wait(relay2(v))
-        par = lax.rem(v, 3)
+        par = lax.rem(v, 3)
+        relays, mains = relay2(v), main2(v)
         for p in range(3):
             for d in range(2):
+                relays[2 * p + d].wait()
                 dst = chunk2(par, p, at_pos((p + 1) % 3, 1 + 2 * d), d)
                 dst[...] = dst[...] + ra2[par, p, d]
-        start(main2(v))
+                mains[2 * p + d].start()
 
     def step_main2(v):
-        wait(main2(v) + direct2(v))
-        par = lax.rem(v, 3)
+        par = lax.rem(v, 3)
+        mains, early, lasts = main2(v), direct2(v), last3(v)
         for p in range(3):
+            pair = slice(2 * p, 2 * p + 2)
+            wait(early[pair] + mains[pair])
             acc3[par, p] = chunk2(par, p, pos[(p + 1) % 3])[...] + rb2[par, p, 0] + rb2[par, p, 1]
-        start(last3(v))
+            start(lasts[3 * p:3 * p + 3])
 
     def step_last3(v):
         wait(last3(v))
@@ -429,7 +438,6 @@
         vmem(TOK, DM, dtype=BF16),
         vmem(NT, TOK, DM, dtype=BF16),
         vmem(TOK, DF, dtype=BF16),
-        vmem(BLK, BLK, dtype=BF16),
         vmem(2, 3, DM, LN),
         vmem(3, *GRID, ROWS, LN),
         vmem(2, *GRID, ROWS, LN),
@@ -445,7 +453,7 @@
         vmem(NL * ROWS, LN),
         vmem(8, 8, LN),
         vmem(16, 8, LN),
-        dma, dma(two + two), dma(three + two), dma(three + two), dma(two), dma(two),
+        dma, dma(two + two), dma(three + two), dma(three + two), dma(two + three), dma(two + three),
         both, both, both, both, both, both, both, both,
         triple, triple, both, both, both, both, dma((7,)), dma((7,)), dma((15,)), dma((15,)),
     ]

time: 186 us -> 182 us (0.978)
  Pallas kernels: 178 us -> 174 us
    pallas_call x1, Pallas kernels: 178 us -> 174 us  [whole_step(): pl.pallas_call(step_kernel, out_shape=(jax.ShapeDtypeStruct((NT,), F32),...]
where the time goes in v4:
time: 182 us
  Pallas kernels  174 us (96%)
  local copies, waits for them, and re-layouts  6.8 us (4%)
    pallas_call x1, Pallas kernels, whole_step(): pl.pallas_call(step_kernel, out_shape=(jax.ShapeDtypeStruct((NT,), F32),...  174 us
    unnamed x4, local copies, waits for them, and re-layouts  5.41 us

profile of v4, /device:TPU:1, one launch (start us, length us, event | category | flops | bytes accessed | tf_op | source)
XLA Modules:
  0.0 181.6 jit_solution(4900987577660933690)
XLA Ops:
  0.6 1.4 pad.4
  2.0 174.1 %shard_map.84 = (f32[3]{0:T(128)}, f32[3,3]{1,0:T(4,128)}, f32[4,4608]{1,0:T(4,128)}, f32[4,4608]{1,0:T(4,128)}, bf16[2,1536,1024]{2,1,0:T(8,128)(2,1)}, /*index...) custom-call(bf16[1024,384]{1,0:T(8,128)(2,1)} %x_hbm.1, s32[3,1024]{1,0:T(4,128)} %lab_ref.1, ...), custom_call_target="tpu_custom_call" | custom-call | tf_op jit(solution)/shard_map/pallas_call | solution.py:460
  176.2 1.1 copy.13
  177.3 1.3 copy.14
  178.5 1.5 copy.15
  180.1 1.5 copy.16

commit v5 on v4

--- a/solution.py
+++ b/solution.py
@@ -33,7 +33,7 @@
 
 
 def step_kernel(x_hbm, lab_ref, w1_hbm, w2_hbm, heads_ref,
-                alpha_ref, gram_ref, up_ref, down_ref, at_save, ht_save, sl_save,
+                pack_ref, at_save, ht_save, sl_save,
                 at, ht, sl, w1, w2, hbuf, dbuf, sbuf, tmp,
                 gown, gsend, rd2d, ra1, rb1, acc2, ra2, rb2, acc3, r3, res, mix, gcore, gax,
                 x_sem, w_sem, save_sem, load_sem, d2d_s, d2d_r, a1_s, a1_r, b1_s, b1_r,
@@ -404,23 +404,23 @@
         return tuple(a / total for a in new)
 
     alpha = lax.fori_loop(0, EG_STEPS, eg_step, tuple(alpha))
+    small = HALF * LN * 2
     for t in range(NT):
-        alpha_ref[t] = alpha[t][0, 0]
+        pack_ref[0:1, small + LN * t:small + LN * (t + 1)] = alpha[t][0:1, :]
         for s in range(NT):
-            gram_ref[t, s] = gram[t, s][0, 0]
+            col = small + LN * (NT + s)
+            pack_ref[t:t + 1, col:col + LN] = gram[t, s][0:1, :]
     scale = [jnp.broadcast_to(alpha[t][0:1, :] * inv_tokens, (72, 128)) for t in range(NT)]
     for layer in range(NL):
         u = NT * (NL - 1 - layer)
         mix[72 * layer:72 * (layer + 1), :] = scale[0] * res[u] + scale[1] * res[u + 1] + scale[2] * res[u + 2]
-    for k in range(36):
-        up_ref[:, LN * k:LN * (k + 1)] = mix[pl.ds(k, NL, stride=ROWS), :]
-        down_ref[:, LN * k:LN * (k + 1)] = mix[pl.ds(36 + k, NL, stride=ROWS), :]
+    for k in range(ROWS):
+        pack_ref[:, LN * k:LN * (k + 1)] = mix[pl.ds(k, NL, stride=ROWS), :]
 
 
 def whole_step(x, labels, w_up, w_down, heads_t):
     any_spec = pl.BlockSpec(memory_space=pl.ANY)
     vmem_spec = pl.BlockSpec(memory_space=pltpu.VMEM)
-    smem_spec = pl.BlockSpec(memory_space=pltpu.SMEM)
     dma = pltpu.SemaphoreType.DMA
     two, three = (2,), (3,)
 
@@ -460,25 +460,26 @@
     return pl.pallas_call(
         step_kernel,
         out_shape=(
-            jax.ShapeDtypeStruct((NT,), F32),
-            jax.ShapeDtypeStruct((NT, NT), F32),
-            jax.ShapeDtypeStruct((NL, HALF * LN), F32),
-            jax.ShapeDtypeStruct((NL, HALF * LN), F32),
+            jax.ShapeDtypeStruct((NL, (ROWS + 2 * NT) * LN), F32),
             jax.ShapeDtypeStruct((2, DF, TOK), BF16),
             jax.ShapeDtypeStruct((2, DM, TOK), BF16),
             jax.ShapeDtypeStruct((2, TOK, DF), F32),
         ),
         in_specs=[any_spec, vmem_spec, any_spec, any_spec, vmem_spec],
-        out_specs=(smem_spec, smem_spec, vmem_spec, vmem_spec, any_spec, any_spec, any_spec),
+        out_specs=(vmem_spec, any_spec, any_spec, any_spec),
         scratch_shapes=scratch,
         compiler_params=pltpu.CompilerParams(
             collective_id=0, has_side_effects=True, vmem_limit_bytes=67043328),
-    )(x, labels, w_up, w_down, heads_t)[:4]
+    )(x, labels, w_up, w_down, heads_t)[0]
 
 
 def solution(mesh):
     def local_step(x_local, lab_local, w_up, w_down, task_heads):
         heads_t = jnp.pad(jnp.swapaxes(task_heads, 1, 2), ((0, 0), (0, 16 - NC), (0, 0))).reshape(NT * 16, DM)
-        return whole_step(x_local, lab_local, w_up, w_down, heads_t)
+        pack = whole_step(x_local, lab_local, w_up, w_down, heads_t)
+        half, small = HALF * LN, 2 * HALF * LN
+        alpha = pack[0, small:small + NT * LN:LN]
+        gram = pack[:NT, small + NT * LN::LN]
+        return alpha, gram, pack[:, :half], pack[:, half:small]
 
     return jax.shard_map(local_step, mesh=mesh, in_specs=(P('data', None), P(None, 'data'), P(), P(), P()), out_specs=(P(), P(), P(None, 'data'), P(None, 'data')), check_vma=False)

time: 182 us -> 181 us (level)
    unnamed x4 -> x0, local copies, waits for them, and re-layouts: 5.41 us -> none
    slice x0 -> x3, local copies, waits for them, and re-layouts: none -> 4.23 us  [the longest x1 1.59 us: local_step(): return (alpha, gram, pack[:, :half], pack[:, half:small])]
where the time goes in v5:
time: 181 us; the launch traced here: 180 us
  Pallas kernels  174 us (96%)
  local copies, waits for them, and re-layouts  5.62 us (3%)
    pallas_call x1, Pallas kernels, whole_step(): pl.pallas_call(step_kernel, out_shape=(jax.ShapeDtypeStruct((NL, (ROWS +...  174 us

profile of v5, /device:TPU:1, one launch (start us, length us, event | category | flops | bytes accessed | tf_op | source)
XLA Modules:
  0.0 180.4 jit_solution(11089955016236458172)
XLA Ops:
  0.6 1.4 pad.4
  2.0 174.1 %shard_map.84 = (f32[4,9984]{1,0:T(4,128)}, bf16[2,1536,1024]{2,1,0:T(8,128)(2,1)}, bf16[2,384,1024]{2,1,0:T(8,128)(2,1)}, f32[2,1024,1536]{2,1,0:T(8,128)}) custom-call(bf16[1024,384]{1,0:T(8,128)(2,1)} %x_hbm.1, s32[3,1024]{1,0:T(4,128)} %lab_ref.1, bf16[4,384,1536]{2,1,0:T(8,128)(2,1)} %w1_hbm.1, bf16[4,1536,384]{2,1,0:T(8,128)(2,1)} %w2_hbm.1, ...), custom_call_target="tpu_custom_call" | custom-call | tf_op jit(solution)/shard_map/pallas_call | solution.py:460
  176.2 1.3 slice.12
  177.4 1.4 slice.13
  178.8 1.6 fusion
